TPU v7x, 8 devices: a whole 2x2x1 slice. The times are simulated.
8 devices in a mesh: dp: 1 (over z), tp: 2 (over y), cp: 4 (over x, core).
Axes of the slice: x: 2, y: 2, z: 1, core: 2. Of those that a mesh axis runs over, the one named last changes fastest.
Arguments:
- hidden_in: bfloat16 [64, 64, 1024], P('dp')
- lengths: int32 [64], P('dp')
- k_cache: bfloat16 [64, 16, 2048, 64], P('dp', 'tp', 'cp')
- v_cache: bfloat16 [64, 16, 2048, 64], P('dp', 'tp', 'cp')
- ln1_gain: float32 [1024], replicated
- ln1_bias: float32 [1024], replicated
- ln2_gain: float32 [1024], replicated
- ln2_bias: float32 [1024], replicated
- w_qkv: bfloat16 [1024, 3072], P(None, 'tp')
- b_qkv: bfloat16 [3072], P('tp')
- w_out: bfloat16 [1024, 1024], P('tp')
- b_out: bfloat16 [1024], replicated
- w_up: bfloat16 [1024, 4096], P(None, 'tp')
- b_up: bfloat16 [4096], P('tp')
- w_down: bfloat16 [4096, 1024], P('tp')
- b_down: bfloat16 [1024], replicated
Outputs:
- output 1: bfloat16 [64, 64, 1024], P('dp')
- output 2: bfloat16 [64, 16, 64, 64], P('dp', 'tp')
- output 3: bfloat16 [64, 16, 64, 64], P('dp', 'tp')
All inputs are finite; a program needn't handle non-finite values.
Results may differ from a plain program's by a relative error of at most 0.00426027.
Values sent between devices are 32-bit elements.
A program may use at most 1 GiB of HBM per device.

v0:
```python
import jax
import jax.numpy as jnp
from jax import lax
from jax.sharding import PartitionSpec as P

EPSILON = 1e-5
NEG_BIG = -1e30
ROTARY_SHARE = 4
ROPE_BASE = 10000.0


def layer_norm(values_in, gain_vec, bias_vec):
    x_f32 = values_in.astype(jnp.float32)
    row_mean = jnp.mean(x_f32, axis=-1, keepdims=True)
    centered = x_f32 - row_mean
    variance = jnp.mean(centered * centered, axis=-1, keepdims=True)
    return (centered * lax.rsqrt(variance + EPSILON) * gain_vec + bias_vec).astype(jnp.bfloat16)


def rotary(values_in, positions):
    head_dim = values_in.shape[-1]
    rot_dim = head_dim // ROTARY_SHARE
    half_rot = rot_dim // 2
    inv_freq = ROPE_BASE ** (-2.0 * jnp.arange(half_rot, dtype=jnp.float32) / rot_dim)
    angles = positions.astype(jnp.float32)[..., None] * inv_freq
    cos_tab = jnp.cos(angles)[..., None, :]
    sin_tab = jnp.sin(angles)[..., None, :]
    rot_first = values_in[..., :half_rot].astype(jnp.float32)
    rot_second = values_in[..., half_rot:rot_dim].astype(jnp.float32)
    new_first = rot_first * cos_tab - rot_second * sin_tab
    new_second = rot_second * cos_tab + rot_first * sin_tab
    return jnp.concatenate([new_first.astype(jnp.bfloat16), new_second.astype(jnp.bfloat16), values_in[..., rot_dim:]], axis=-1)


def cache_piece(q_rot, k_slots, v_slots, slot_ids, lengths):
    head_dim = q_rot.shape[3]
    slot_valid = (slot_ids[None, :] < lengths[:, None])[:, None, None, :]
    scores = jnp.einsum("bchd,bhsd->bhcs", q_rot, k_slots, preferred_element_type=jnp.float32) * head_dim ** -0.5
    scores = jnp.where(slot_valid, scores, NEG_BIG)
    piece_max = scores.max(axis=-1)
    probs = jnp.where(slot_valid, jnp.exp(scores - piece_max[..., None]), 0.0)
    piece_out = jnp.einsum("bhcs,bhsd->bhcd", probs.astype(jnp.bfloat16), v_slots, preferred_element_type=jnp.float32)
    return piece_max, probs.sum(axis=-1), piece_out


def self_piece(q_chunk, k_chunk, v_chunk):
    chunk_len = q_chunk.shape[1]
    head_dim = q_chunk.shape[3]
    causal = jnp.arange(chunk_len)[:, None] >= jnp.arange(chunk_len)[None, :]
    scores = jnp.einsum("bchd,bkhd->bhck", q_chunk, k_chunk, preferred_element_type=jnp.float32) * head_dim ** -0.5
    scores = jnp.where(causal, scores, NEG_BIG)
    piece_max = scores.max(axis=-1)
    probs = jnp.where(causal, jnp.exp(scores - piece_max[..., None]), 0.0)
    piece_out = jnp.einsum("bhck,bkhd->bhcd", probs.astype(jnp.bfloat16), v_chunk, preferred_element_type=jnp.float32)
    return piece_max, probs.sum(axis=-1), piece_out


def empty_piece(q_chunk, k_chunk, v_chunk):
    num_rows, chunk_len, heads_here, head_dim = q_chunk.shape
    stat_shape = (num_rows, heads_here, chunk_len)
    return (jnp.full(stat_shape, NEG_BIG, jnp.float32), jnp.zeros(stat_shape, jnp.float32), jnp.zeros(stat_shape + (head_dim,), jnp.float32))


def solution(mesh):
    in_specs = (P("dp", None, None), P("dp"), P("dp", "tp", "cp", None), P("dp", "tp", "cp", None), P(), P(), P(), P(), P(None, "tp"), P("tp"), P("tp", None), P(), P(None, "tp"), P("tp"), P("tp", None), P())
    out_specs = (P("dp", None, None), P("dp", "tp", None, None), P("dp", "tp", None, None))

    def local_layer(hidden_in, lengths, k_block, v_block, ln1_gain, ln1_bias, ln2_gain, ln2_bias, w_qkv, b_qkv, w_out, b_out, w_up, b_up, w_down, b_down):
        num_rows, chunk_len, d_model = hidden_in.shape
        heads_here = k_block.shape[1]
        block_len = k_block.shape[2]
        head_dim = k_block.shape[3]
        cp_index = lax.axis_index("cp")
        normed_attn = layer_norm(hidden_in, ln1_gain, ln1_bias)
        normed_mlp = layer_norm(hidden_in, ln2_gain, ln2_bias)
        qkv_all = (jnp.einsum("bcd,de->bce", normed_attn, w_qkv, preferred_element_type=jnp.float32) + b_qkv.astype(jnp.float32)).astype(jnp.bfloat16)
        qkv_all = qkv_all.reshape(num_rows, chunk_len, heads_here, 3, head_dim)
        positions = lengths[:, None] + jnp.arange(chunk_len, dtype=jnp.int32)[None, :]
        q_rot = rotary(qkv_all[:, :, :, 0], positions)
        k_rot = rotary(qkv_all[:, :, :, 1], positions)
        v_chunk = qkv_all[:, :, :, 2]
        slot_ids = cp_index * block_len + jnp.arange(block_len, dtype=jnp.int32)
        cache_max, cache_sum, cache_out = cache_piece(q_rot, k_block, v_block, slot_ids, lengths)
        own_max, own_sum, own_out = lax.cond(cp_index == 0, self_piece, empty_piece, q_rot, k_rot, v_chunk)
        global_max = lax.pmax(jnp.maximum(cache_max, own_max), "cp")
        cache_weight = jnp.exp(cache_max - global_max)
        own_weight = jnp.exp(own_max - global_max)
        out_part = cache_out * cache_weight[..., None] + own_out * own_weight[..., None]
        sum_part = cache_sum * cache_weight + own_sum * own_weight
        out_total, sum_total = lax.psum((out_part, sum_part), "cp")
        context = (out_total / sum_total[..., None]).astype(jnp.bfloat16)
        attn_part = jnp.einsum("bhcd,hde->bce", context, w_out.reshape(heads_here, head_dim, d_model), preferred_element_type=jnp.float32)
        hidden = jax.nn.gelu(jnp.einsum("bcd,df->bcf", normed_mlp, w_up, preferred_element_type=jnp.float32) + b_up.astype(jnp.float32), approximate=False).astype(jnp.bfloat16)
        mlp_part = jnp.einsum("bcf,fd->bcd", hidden, w_down, preferred_element_type=jnp.float32)
        branch_sum = lax.psum(attn_part + mlp_part, "tp")
        out_sum = hidden_in.astype(jnp.float32) + branch_sum + b_out.astype(jnp.float32) + b_down.astype(jnp.float32)
        return out_sum.astype(jnp.bfloat16), jnp.swapaxes(k_rot, 1, 2), jnp.swapaxes(v_chunk, 1, 2)

    return jax.shard_map(local_layer, mesh=mesh, in_specs=in_specs, out_specs=out_specs, check_vma=False)
```

profile of v0, /device:TPU:1, one launch (start us, length us, event | category | flops | bytes accessed | tf_op | source)
XLA Modules:
  0.0 1130.5 jit_solution(12830751189832917970)
XLA Ops:
  7.2 0.0 copy-start
  7.2 0.0 copy-start.7
  7.2 0.0 copy-start.14
  7.2 0.0 copy-start.13
  7.2 0.0 all-reduce.5.cloned.1.call-start
  7.3 0.0 slice-start
  7.3 4.7 convert_reduce_fusion
  12.0 0.0 copy-start.3
  12.0 0.0 slice-start.1
  12.0 5.6 fusion.42
  17.6 0.0 copy-done.7
  17.6 0.0 copy-start.5
  17.6 0.0 copy-done.3
  17.6 0.6 copy-done.5
  18.2 0.0 copy-done
  18.2 0.0 copy-done.14
  18.2 0.0 copy-done.13
  18.2 0.0 slice-done
  18.2 0.0 slice-done.1
  18.2 15.8 %add_convert_fusion = bf16[64,64,1536]{2,1,0:T(8,128)(2,1)} fusion(f32[1536]{0:T(1024)S(1)} %convert_element_type.78, bf16[64,64,1024]{2,1,0:T(8,128)(2,1)S(1)} %bitcast.41, f32[1024]{0:T(1024)S(1)} %copy-done.13, f32[1024]{0:T(1024)S(1)} %copy-done.14, f32[64,64]{1,0:T(8,128)S(1)} %add_rsqrt_fusion, f32[64,64]{1,0:T(8,128)S(1)} %broadcast_multiply_fusion, ...), kind=kOutput, calls=%fused_computation.46 | convolution fusion | flops 12922650624 | bytes 24164352 | tf_op jit(solution)/shard_map/bcd,de->bce/dot_general | solution.py:76
  34.0 62.6 %reshape.92 = bf16[64,64,8,3,64]{4,3,2,1,0:T(4,128)(2,1)} reshape(bf16[64,64,1536]{2,1,0:T(8,128)(2,1)} %add_convert_fusion) | data formatting | bytes 25165824 | tf_op jit(solution)/shard_map/reshape | solution.py:77
  96.6 53.9 %fusion.117 = (bf16[64,64,8,1,64]{4,3,2,1,0:T(2,128)(2,1)}, bf16[64,64,8,1,64]{4,3,2,1,0:T(2,128)(2,1)}, bf16[64,64,8,1,64]{4,3,2,1,0:T(2,128)(2,1)}) fusion(bf16[64,64,8,3,64]{4,3,2,1,0:T(4,128)(2,1)} %reshape.92), kind=kLoop, calls=%fused_computation.145 | loop fusion | bytes 25165824 | tf_op jit(solution)/shard_map/slice | solution.py:81
  150.5 32.7 %copy.48 = bf16[64,64,8,1,64]{1,4,2,0,3:T(8,128)(2,1)} copy(bf16[64,64,8,1,64]{4,3,2,1,0:T(2,128)(2,1)} %get-tuple-element.44) | data formatting | bytes 8388608
  183.2 32.7 %copy.49 = bf16[64,64,8,1,64]{1,4,2,0,3:T(8,128)(2,1)} copy(bf16[64,64,8,1,64]{4,3,2,1,0:T(2,128)(2,1)} %get-tuple-element.45) | data formatting | bytes 8388608
  215.9 0.0 copy-done.9
  215.9 0.1 add_convert_fusion.1
  216.0 7.5 slice.39
  223.5 0.0 copy-done.2
  223.5 4.4 slice.43
  227.9 10.8 copy.56
  238.7 0.1 broadcast_compare_fusion
  238.8 1.0 multiply_cosine_fusion
  239.8 5.3 fusion.79
  245.1 37.5 %fusion.14 = (f32[64,8,64]{2,1,0:T(8,128)S(1)}, f32[64,8,64,512]{3,2,1,0:T(8,128)}) fusion(pred[64,512]{1,0:T(8,128)(4,1)S(1)} %broadcast_compare_fusion, bf16[64,8,512,64]{2,3,1,0:T(8,128)(2,1)} %param.20, bf16[64,64,8,48]{1,3,2,0:T(8,128)(2,1)} %slice.39, bf16[64,64,8,8]{1,3,2,0:T(8,128)(2,1)S(1)} %get-tuple-element.52, ...), kind=kOutput, calls=%fused_computation.18 | convolution fusion | flops 2210365440 | bytes 105021440 | tf_op jit(solution)/shard_map/bchd,bhsd->bhcs/dot_general | solution.py:38
  282.6 14.7 %fusion.115 = (bf16[64,8,64,64]{2,3,1,0:T(8,128)(2,1)}, bf16[64,64,8,64]{1,3,2,0:T(8,128)(2,1)}, bf16[64,64,8,64]{1,3,2,0:T(8,128)(2,1)}) fusion(bf16[64,64,8,48]{1,3,2,0:T(8,128)(2,1)} %slice.43, bf16[64,64,8,8]{1,3,2,0:T(8,128)(2,1)} %get-tuple-element.47, bf16[64,64,8,8]{1,3,2,0:T(8,128)(2,1)} %get-tuple-element.46, bf16[64,64,8,48]{1,3,2,0:T(8,128)(2,1)} %slice.39, ...), kind=kLoop, calls=%fused_computation.143 | loop fusion | flops 25165824 | bytes 20971520 | tf_op jit(solution)/shard_map/transpose | solution.py:97
  297.3 8.6 conditional.1
  297.3 7.9 broadcast.108
  305.2 0.7 broadcast.106
  306.0 1.7 max.5
  307.6 0.0 all-reduce.5.cloned.1.call-update
  307.7 0.0 all-reduce.9.cloned.1.call-start
  307.7 0.0 copy-start.8
  307.7 21.6 %fusion.15 = f32[64,8,64]{2,1,0:T(8,128)S(1)} fusion(f32[64,8,64,512]{3,2,1,0:T(8,128)} %get-tuple-element.57, f32[64,8,64]{2,1,0:T(8,128)S(1)} %get-tuple-element.56, pred[64,512]{1,0:T(8,128)(4,1)S(1)} %broadcast_compare_fusion), kind=kLoop, calls=%fused_computation.20 | loop fusion | flops 83853312 | bytes 67403776 | tf_op jit(solution)/shard_map/reduce_sum | solution.py:43
  329.4 31.1 %all-reduce.5.cloned.1.call-done = f32[64,8,64]{2,1,0:T(8,128)} async-done(((f32[64,8,64]{2,1,0:T(8,128)}), f32[64,8,64]{2,1,0:T(8,128)}) %all-reduce.5.cloned.1.call-update) | async-done | bytes 131088 | tf_op jit(solution)/shard_map/pmax | solution.py:85
  360.4 1.8 multiply_add_fusion.1
  362.3 43.7 %multiply_add_fusion = f32[64,8,64,64]{3,2,1,0:T(8,128)} fusion(f32[64,8,64,64]{3,2,1,0:T(8,128)} %get-tuple-element.16, bf16[64,8,512,64]{2,3,1,0:T(8,128)(2,1)} %param.21, f32[64,8,64,512]{3,2,1,0:T(8,128)} %get-tuple-element.57, f32[64,8,64]{2,1,0:T(8,128)S(1)} %get-tuple-element.56, pred[64,512]{1,0:T(8,128)(4,1)S(1)} %broadcast_compare_fusion, ...), kind=kOutput, calls=%fused_computation.64 | convolution fusion | flops 2237661184 | bytes 117866496 | tf_op jit(solution)/shard_map/bhcs,bhsd->bhcd/dot_general | solution.py:42
  406.0 0.0 copy-start.16
  406.0 0.0 all-reduce.9.cloned.1.call-update
  406.0 0.4 all-reduce.7.cloned.1.call-start
  406.5 0.3 copy-done.4
  406.7 0.0 copy-done.6
  406.8 0.0 copy-done.16
  406.8 93.6 %fusion.135 = bf16[64,64,2048]{2,1,0:T(8,128)(2,1)} fusion(f32[2048]{0:T(1024)S(1)} %convert_element_type.93, bf16[64,64,1024]{2,1,0:T(8,128)(2,1)} %param.18, f32[1024]{0:T(1024)S(1)} %copy-done.15, f32[1024]{0:T(1024)S(1)} %copy-done.16, f32[64,64]{1,0:T(8,128)S(1)} %copy-done.6, f32[64,64]{1,0:T(8,128)S(1)} %copy-done.4, ...), kind=kOutput, calls=%fused_computation.25.clone.clone.clone.clone.1 | convolution fusion | flops 17758683136 | bytes 29409280 | tf_op jit(solution)/shard_map/bcd,df->bcf/dot_general | solution.py:93
  500.3 194.8 %all-reduce.9.cloned.1.call-done = (f32[64,8,64,64]{3,2,1,0:T(8,128)}, f32[64,8,64]{2,1,0:T(8,128)}) async-done(((f32[64,8,64,64]{3,2,1,0:T(8,128)}, f32[64,8,64]{2,1,0:T(8,128)}), (f32[64,8,64,64]{3,2,1,0:T(8,128)}, f32[64,8,64]{2,1,0:T(8,128)})) %all-reduce.9.cloned.1.call-update) | async-done | bytes 8519696 | tf_op jit(solution)/shard_map/psum | solution.py:90
  695.1 15.9 %fusion.69 = f32[64,64,1024,1]{2,1,3,0:T(8,128)} fusion(bf16[8,64,1024,1]{2,1,0,3:T(8,128)(2,1)S(1)} %bitcast.48, f32[64,8,64,64]{3,2,1,0:T(8,128)} %get-tuple-element.36, f32[64,8,64]{2,1,0:T(8,128)} %get-tuple-element.37), kind=kOutput, calls=%fused_computation.79 | convolution fusion | flops 4299161600 | bytes 26345472 | tf_op jit(solution)/shard_map/bhcd,hde->bce/dot_general | solution.py:92
  711.0 28.1 %bitcast_add_fusion = f32[64,64,1024]{2,1,0:T(8,128)} fusion(f32[64,64,1024,1]{2,1,3,0:T(8,128)} %fusion.69, bf16[2048,1024]{1,0:T(8,128)(2,1)} %param.32, bf16[64,64,2048]{2,1,0:T(8,128)(2,1)} %fusion.135), kind=kOutput, calls=%fused_computation.62 | convolution fusion | flops 17184063488 | bytes 54525952 | tf_op jit(solution)/shard_map/bcf,fd->bcd/dot_general | solution.py:94
  739.1 0.0 all-reduce.7.cloned.1.call-update
  739.1 0.0 copy-start.10
  739.1 0.0 copy-start.11
  739.1 12.1 %copy.55 = bf16[64,64,8,1,64]{4,1,2,0,3:T(8,128)(2,1)} copy(bf16[64,64,8,1,64]{4,3,2,1,0:T(2,128)(2,1)} %get-tuple-element.43) | data formatting | bytes 8388608 | tf_op jit(solution)/shard_map/transpose | solution.py:97
  751.3 0.0 copy-start.1
  751.3 12.0 %copy.40 = bf16[64,8,64,64]{3,2,1,0:T(8,128)(2,1)} copy(bf16[64,8,64,64]{2,3,1,0:T(8,128)(2,1)} %get-tuple-element.50) | data formatting | bytes 8388608
  763.3 348.3 %all-reduce.7.cloned.1.call-done = f32[64,64,1024]{2,1,0:T(8,128)} async-done(((f32[64,64,1024]{2,1,0:T(8,128)}), f32[64,64,1024]{2,1,0:T(8,128)}) %all-reduce.7.cloned.1.call-update) | async-done | bytes 16777232 | tf_op jit(solution)/shard_map/psum | solution.py:95
  1111.6 12.2 %fusion.45 = bf16[64,64,1024]{2,1,0:T(8,128)(2,1)} fusion(f32[64,64,1024]{2,1,0:T(8,128)} %all-reduce.7.cloned.1.call-done, bf16[64,64,1024]{2,1,0:T(8,128)(2,1)} %param.18, f32[1024]{0:T(1024)S(1)} %convert_element_type.96, f32[1024]{0:T(1024)S(1)} %convert_element_type.95), kind=kLoop, calls=%fused_computation.61 | loop fusion | flops 20971520 | bytes 33562624 | tf_op jit(solution)/shard_map/convert_element_type | solution.py:97
  (22 shorter events, 0.1 us)
Async XLA Ops:
  7.2 11.1 copy-start
  7.2 10.4 copy-start.7
  7.2 11.0 copy-start.14
  7.2 11.0 copy-start.13
  7.2 353.2 %all-reduce.5.cloned.1.call-start = ((), (), s32[]{:S(2)}) async-start(), calls=%async_computation | async-start | bytes 524288 | tf_op jit(solution)/shard_map/pmax | solution.py:85
  7.3 11.0 slice-start
  12.0 5.7 copy-start.3
  12.0 6.2 slice-start.1
  17.6 0.6 copy-start.5
  183.2 32.7 %copy-start.9 = (s32[64]{0:T(128)S(1)}, s32[64]{0:T(128)}, u32[]{:S(2)}) copy-start(s32[64]{0:T(128)} %param.19) | copy-start | bytes 772
  215.9 7.6 copy-start.2
  307.7 387.4 %all-reduce.9.cloned.1.call-start = ((), (), s32[]{:S(2)}) async-start(), calls=%async_computation.2 | async-start | bytes 34078720 | tf_op jit(solution)/shard_map/psum | solution.py:90
  307.7 21.7 %copy-start.8 = (bf16[2048]{0:T(1024)(128)(2,1)S(1)}, bf16[2048]{0:T(1024)(128)(2,1)}, u32[]{:S(2)}) copy-start(bf16[2048]{0:T(1024)(128)(2,1)} %param.31) | copy-start | bytes 12292
  406.0 0.8 copy-start.4
  406.0 0.8 copy-start.6
  406.0 0.8 copy-start.15
  406.0 0.8 copy-start.16
  406.0 705.6 %all-reduce.7.cloned.1.call-start = ((), (), s32[]{:S(2)}) async-start(), calls=%async_computation.1 | async-start | bytes 33554432 | tf_op jit(solution)/shard_map/psum | solution.py:95
  406.8 288.4 %copy-start.12 = (bf16[512,1024]{1,0:T(8,128)(2,1)S(1)}, bf16[512,1024]{1,0:T(8,128)(2,1)}, u32[]{:S(2)}) copy-start(bf16[512,1024]{1,0:T(8,128)(2,1)} %param.28) | copy-start | bytes 3145732
  739.1 12.2 %copy-start.10 = (bf16[1024]{0:T(1024)(128)(2,1)S(1)}, bf16[1024]{0:T(1024)(128)(2,1)}, u32[]{:S(2)}) copy-start(bf16[1024]{0:T(1024)(128)(2,1)} %param.29) | copy-start | bytes 6148
  739.1 12.1 %copy-start.11 = (bf16[1024]{0:T(1024)(128)(2,1)S(1)}, bf16[1024]{0:T(1024)(128)(2,1)}, u32[]{:S(2)}) copy-start(bf16[1024]{0:T(1024)(128)(2,1)} %param.33) | copy-start | bytes 6148
  751.3 372.5 %copy-start.1 = (bf16[1024,1536]{1,0:T(8,128)(2,1)S(1)}, bf16[1024,1536]{1,0:T(8,128)(2,1)}, u32[]{:S(2)}) copy-start(bf16[1024,1536]{1,0:T(8,128)(2,1)} %param.26) | copy-start | bytes 9437188
Sparse Core Ops, SparseCore 0:
  307.8 52.6 all-reduce.4
  406.1 288.9 all-reduce.8
  739.2 372.3 all-reduce.6
where the time goes:
time: 1140 us; the launch traced here: 1130 us
  waiting for transfers between devices  574 us (50%)
  local copies, waits for them, and re-layouts  238 us (21%)
  matrix products  235 us (21%)
  other arithmetic  68.8 us (6%)
  between operations  14.2 us (1%)
    psum x1, waiting for transfers between devices, local_layer(): branch_sum = lax.psum(attn_part + mlp_part, 'tp')  348 us
    psum x1, waiting for transfers between devices, local_layer(): out_total, sum_total = lax.psum((out_part, sum_part), 'cp')  195 us
    dot_general x1, matrix products, local_layer(): jnp.einsum('bcd,df->bcf', normed_mlp, w_up, preferred_element_type=jnp.fl...  93.6 us
    unnamed x42, local copies, waits for them, and re-layouts  89.1 us
    reshape x1, local copies, waits for them, and re-layouts, local_layer(): qkv_all = qkv_all.reshape(num_rows, chunk_len, heads_here, 3, head_dim)  62.6 us
    slice x1, local copies, waits for them, and re-layouts, local_layer(): v_chunk = qkv_all[:, :, :, 2]  53.9 us
    dot_general x1, matrix products, cache_piece(): jnp.einsum('bhcs,bhsd->bhcd', probs.astype(jnp.bfloat16), v_slots, prefer...  43.7 us
    dot_general x1, matrix products, cache_piece(): jnp.einsum('bchd,bhsd->bhcs', q_rot, k_slots, preferred_element_type=jnp....  37.5 us
  transfers between devices with their start and end apart: 3, of which 3 were waited for; matrix products, arithmetic and copies ran while one was open for 12% of the time, Pallas kernels for 0%

commit v1 on v0

v1 whole, which is shorter than its diff:
```python
import functools
import numpy as np
import jax
import jax.numpy as jnp
from jax import lax
from jax.experimental import pallas as pl
from jax.experimental.pallas import tpu as pltpu
from jax.sharding import PartitionSpec as P

EPSILON = 1e-5
NEG_BIG = -1e30
MAX_FLOOR = -1e29
ROPE_BASE = 10000.0
HEAD_DIM = 64
ROT_DIM = 16
PAIR = 2 * HEAD_DIM
ROWS = 64
CHUNK = 64
HEADS = 8
WIDTH = HEADS * HEAD_DIM
SLOTS = 512
D_MODEL = 1024
FF = 2048
GROUP = 8
GROUPS = ROWS // GROUP
KV_BUFS = 3
QKV_ROWS = 4
QKV_TOKENS = QKV_ROWS * CHUNK
F32 = jnp.float32
BF16 = jnp.bfloat16
ANY = pl.BlockSpec(memory_space=pl.ANY)


def normalize(x_f32, gain, bias):
    row_mean = jnp.mean(x_f32, axis=-1, keepdims=True)
    centered = x_f32 - row_mean
    variance = jnp.mean(centered * centered, axis=-1, keepdims=True)
    return (centered * lax.rsqrt(variance + EPSILON) * gain + bias).astype(BF16)


def rotate_matrix():
    matrix = np.zeros((PAIR, PAIR), np.float32)
    half = ROT_DIM // 2
    for base in (0, HEAD_DIM):
        for i in range(half):
            matrix[base + half + i, base + i] = -1.0
            matrix[base + i, base + half + i] = 1.0
    return matrix


def qkv_kernel(len_ref, x_ref, gain_ref, bias_ref, w_ref, bq_ref, freq_ref, rot_ref, q_out, k_out, v_out, kd_out, vd_out, w_perm):
    step = pl.program_id(0)

    @pl.when(step == 0)
    def _():
        for part in range(3):
            for pair in range(HEADS // 2):
                first = 2 * pair * 3 * HEAD_DIM + part * HEAD_DIM
                second = first + 3 * HEAD_DIM
                w_perm[:, part * WIDTH + pair * PAIR:part * WIDTH + (pair + 1) * PAIR] = jnp.concatenate([w_ref[:, first:first + HEAD_DIM], w_ref[:, second:second + HEAD_DIM]], axis=1)

    normed = normalize(x_ref[...].astype(F32), gain_ref[...], bias_ref[...])
    lane_token = lax.broadcasted_iota(jnp.int32, (ROT_DIM // 2, QKV_TOKENS), 1)
    base = jnp.zeros((ROT_DIM // 2, QKV_TOKENS), jnp.int32)
    for row in range(QKV_ROWS):
        base = jnp.where(lane_token // CHUNK == row, len_ref[step * QKV_ROWS + row], base)
    angles = (base + lane_token % CHUNK).astype(F32) * freq_ref[:, 0:1]
    cos8 = jnp.cos(angles)
    sin8 = jnp.sin(angles)
    rest = HEAD_DIM - ROT_DIM
    ones = jnp.ones((rest, QKV_TOKENS), F32)
    zeros = jnp.zeros((rest, QKV_TOKENS), F32)
    cos_tab = jnp.concatenate([cos8, cos8, ones, cos8, cos8, ones], axis=0).T
    sin_tab = jnp.concatenate([sin8, sin8, zeros, sin8, sin8, zeros], axis=0).T

    def section(part):
        cols = pl.ds(part * WIDTH, WIDTH)
        return (jnp.dot(normed, w_perm[:, cols], preferred_element_type=F32) + bq_ref[:, cols]).astype(BF16)

    def turn(values):
        pieces = []
        for pair in range(HEADS // 2):
            x = values[:, pair * PAIR:(pair + 1) * PAIR]
            turned = jnp.dot(x, rot_ref[...], preferred_element_type=F32)
            pieces.append(x.astype(F32) * cos_tab + turned * sin_tab)
        return pieces

    q_parts = turn(section(0))
    for pair in range(HEADS // 2):
        q_out[:, pair * PAIR:(pair + 1) * PAIR] = (q_parts[pair] * (HEAD_DIM ** -0.5)).astype(BF16)
    k_parts = turn(section(1))
    v_all = section(2)
    vd_out[...] = v_all
    for pair in range(HEADS // 2):
        k_pair = k_parts[pair].astype(BF16)
        kd_out[:, pair * PAIR:(pair + 1) * PAIR] = k_pair
        v_pair = v_all[:, pair * PAIR:(pair + 1) * PAIR]
        for row in range(QKV_ROWS):
            tokens = slice(row * CHUNK, (row + 1) * CHUNK)
            for sub in range(2):
                dims = slice(sub * HEAD_DIM, (sub + 1) * HEAD_DIM)
                k_out[row, 2 * pair + sub] = k_pair[tokens, dims]
                v_out[row, 2 * pair + sub] = v_pair[tokens, dims]


def qkv_call(lengths, x_flat, gain, bias, w_qkv, b_perm, freq, rot):
    tokens = ROWS * CHUNK
    steps = ROWS // QKV_ROWS
    whole = lambda shape: pl.BlockSpec(shape, lambda i: (0,) * len(shape))
    dense = pl.BlockSpec((QKV_TOKENS, WIDTH), lambda i: (i, 0))
    heads = pl.BlockSpec((QKV_ROWS, HEADS, CHUNK, HEAD_DIM), lambda i: (i, 0, 0, 0))
    return pl.pallas_call(
        qkv_kernel,
        grid=(steps,),
        in_specs=[
            pl.BlockSpec(memory_space=pltpu.SMEM),
            pl.BlockSpec((QKV_TOKENS, D_MODEL), lambda i: (i, 0)),
            whole((1, D_MODEL)), whole((1, D_MODEL)), whole((D_MODEL, 3 * WIDTH)), whole((1, 3 * WIDTH)),
            whole((ROT_DIM // 2, 128)), whole((PAIR, PAIR)),
        ],
        out_specs=[dense, heads, heads, dense, dense],
        out_shape=[
            jax.ShapeDtypeStruct((tokens, WIDTH), BF16),
            jax.ShapeDtypeStruct((ROWS, HEADS, CHUNK, HEAD_DIM), BF16),
            jax.ShapeDtypeStruct((ROWS, HEADS, CHUNK, HEAD_DIM), BF16),
            jax.ShapeDtypeStruct((tokens, WIDTH), BF16),
            jax.ShapeDtypeStruct((tokens, WIDTH), BF16),
        ],
        scratch_shapes=[pltpu.VMEM((D_MODEL, 3 * WIDTH), BF16)],
        cost_estimate=pl.CostEstimate(flops=2 * tokens * D_MODEL * 3 * WIDTH, bytes_accessed=40 << 20, transcendentals=0),
        name="qkv",
    )(lengths, x_flat, gain, bias, w_qkv, b_perm, freq, rot)


def layer_kernel(len_ref, q_hbm, kd_hbm, vd_hbm, kc_hbm, vc_hbm, x_hbm, gain_ref, bias_ref, wo_hbm, wu_hbm, bu_ref, wd_hbm, bo_ref, bd_ref, out_hbm,
                 wo, wu, wd, kbuf, vbuf, qbuf, self_buf, x_buf, o_buf, stat, c_recv, c_stat, cx_stat, x_recv, x_stat, ctx, y_send, y_keep, y_recv, fin, stage,
                 w_sem, kv_sem, self_sem, c_ssem, c_rsem, x_ssem, x_rsem, y_ssem, y_rsem, f_ssem, f_rsem, out_sem):
    tp_id = lax.axis_index("tp")
    cp_id = lax.axis_index("cp")
    chip_x = cp_id // 2
    core = cp_id % 2
    to_core = {"cp": 2 * chip_x + 1 - core}
    to_x = {"cp": 2 * (1 - chip_x) + core}
    to_y = {"tp": 1 - tp_id}

    def flip(bit, mine):
        return bit + mine - 2 * bit * mine

    def row_of(group, slot):
        return group * GROUP + 4 * flip(slot // 4, core) + 2 * flip((slot // 2) % 2, chip_x) + flip(slot % 2, tp_id)

    def remote(src, dst, ssem, rsem, device):
        return pltpu.make_async_remote_copy(src_ref=src, dst_ref=dst, send_sem=ssem, recv_sem=rsem, device_id=device, device_id_type=pl.DeviceIdType.MESH)

    def kv_copies(n):
        b = n % KV_BUFS
        row = row_of(n // GROUP, (n % GROUP + 4) % GROUP)
        return (pltpu.make_async_copy(kc_hbm.at[row], kbuf.at[b], kv_sem.at[b, 0]), pltpu.make_async_copy(vc_hbm.at[row], vbuf.at[b], kv_sem.at[b, 1]), pltpu.make_async_copy(q_hbm.at[row], qbuf.at[b], kv_sem.at[b, 2]))

    def self_copies(g):
        b = g % 2
        copies = []
        for slot in range(2):
            row = row_of(g, slot)
            for k, src in enumerate((q_hbm, kd_hbm, vd_hbm)):
                copies.append(pltpu.make_async_copy(src.at[row], self_buf.at[b, slot, k], self_sem.at[b, slot * 4 + k]))
            copies.append(pltpu.make_async_copy(x_hbm.at[row], x_buf.at[b, slot], self_sem.at[b, slot * 4 + 3]))
        return copies

    w_copies = (pltpu.make_async_copy(wo_hbm, wo, w_sem.at[0]), pltpu.make_async_copy(wu_hbm, wu, w_sem.at[1]), pltpu.make_async_copy(wd_hbm, wd, w_sem.at[2]))

    def c_copies(g):
        return (remote(o_buf.at[g, pl.ds(4, 4)], c_recv.at[g], c_ssem.at[g, 0], c_rsem.at[g, 0], to_core), remote(stat.at[g, 0], c_stat.at[g], c_ssem.at[g, 1], c_rsem.at[g, 1], to_core))

    def x_copies(g):
        return (remote(o_buf.at[g, pl.ds(2, 2)], x_recv.at[g], x_ssem.at[g, 0], x_rsem.at[g, 0], to_x), remote(cx_stat.at[g], x_stat.at[g], x_ssem.at[g, 1], x_rsem.at[g, 1], to_x))

    def y_copy(g):
        return remote(y_send.at[g], y_recv.at[g], y_ssem.at[g], y_rsem.at[g], to_y)

    def f_copy(g, src, dst, k, device):
        return remote(fin.at[g, src], fin.at[g, dst], f_ssem.at[g, k], f_rsem.at[g, dst], device)

    def out_copy(g, slot):
        return pltpu.make_async_copy(stage.at[g % 2, slot], out_hbm.at[row_of(g, slot)], out_sem.at[g % 2, slot])

    lane = lax.broadcasted_iota(jnp.int32, (CHUNK, PAIR), 1)
    low_half = lane < HEAD_DIM
    is_max = lane % 16 < 8

    def stacked_heads(q_pair):
        zero = jnp.zeros_like(q_pair)
        return jnp.concatenate([jnp.where(low_half, q_pair, zero), jnp.where(low_half, zero, q_pair)], axis=0)

    def spread(weights, column):
        return jnp.where(low_half, weights[:, column:column + 1], weights[:, column + 1:column + 2])

    def attend(g, j):
        n = g * GROUP + j
        slot = (j + 4) % GROUP
        b = n % KV_BUFS
        for copy in kv_copies(n):
            copy.wait()

        @pl.when(n + KV_BUFS - 1 < ROWS)
        def _():
            for copy in kv_copies(n + KV_BUFS - 1):
                copy.start()

        row_len = len_ref[row_of(g, slot)]
        slot_ids = cp_id * SLOTS + lax.broadcasted_iota(jnp.int32, (PAIR, SLOTS), 1)
        valid = slot_ids < row_len
        packed = stat[g, j // 4]
        for pair in range(HEADS // 2):
            cols = slice(pair * PAIR, (pair + 1) * PAIR)
            q2 = stacked_heads(qbuf[b, :, cols])
            scores = jnp.where(valid, jnp.dot(q2, kbuf[b, cols, :], preferred_element_type=F32), NEG_BIG)
            top = jnp.maximum(jnp.max(scores, axis=1, keepdims=True), MAX_FLOOR)
            probs = jnp.exp(scores - top)
            total = jnp.sum(probs, axis=1, keepdims=True)
            both = lax.dot_general(probs.astype(BF16), vbuf[b, cols, :], (((1,), (1,)), ((), ())), preferred_element_type=F32)
            o_buf[g, slot, :, cols] = jnp.where(low_half, both[:CHUNK], both[CHUNK:])
            for sub in range(2):
                column = slot % 4 * 16 + 2 * pair + sub
                rows = slice(sub * CHUNK, (sub + 1) * CHUNK)
                packed = jnp.where(lane == column, top[rows], packed)
                packed = jnp.where(lane == column + 8, total[rows], packed)
        stat[g, j // 4] = packed

    def core_stage(g):
        for copy in c_copies(g):
            copy.wait_recv()
        mine = stat[g, 1]
        theirs = c_stat[g]
        top = jnp.maximum(mine, theirs)
        w_mine = jnp.exp(mine - top)
        w_theirs = jnp.exp(theirs - top)
        total = mine * pltpu.roll(w_mine, 8, 1) + theirs * pltpu.roll(w_theirs, 8, 1)
        cx_stat[g] = jnp.where(is_max, top, total)
        for slot in (2, 3, 0, 1):
            for pair in range(HEADS // 2):
                cols = slice(pair * PAIR, (pair + 1) * PAIR)
                column = slot * 16 + 2 * pair
                o_buf[g, slot, :, cols] = o_buf[g, slot, :, cols] * spread(w_mine, column) + c_recv[g, slot, :, cols] * spread(w_theirs, column)
            if slot == 3:
                for copy in x_copies(g):
                    copy.start()

    def x_stage(g):
        b = g % 2
        for copy in self_copies(g):
            copy.wait()
        packed = jnp.where(is_max, NEG_BIG, 0.0)
        causal = lax.broadcasted_iota(jnp.int32, (PAIR, CHUNK), 0) % CHUNK >= lax.broadcasted_iota(jnp.int32, (PAIR, CHUNK), 1)
        own = {}
        for slot in range(2):
            for pair in range(HEADS // 2):
                cols = slice(pair * PAIR, (pair + 1) * PAIR)
                q2 = stacked_heads(self_buf[b, slot, 0, :, cols])
                scores = lax.dot_general(q2, self_buf[b, slot, 1, :, cols], (((1,), (1,)), ((), ())), preferred_element_type=F32)
                scores = jnp.where(causal, scores, NEG_BIG)
                top = jnp.max(scores, axis=1, keepdims=True)
                probs = jnp.where(causal, jnp.exp(scores - top), 0.0)
                total = jnp.sum(probs, axis=1, keepdims=True)
                both = jnp.dot(probs.astype(BF16), self_buf[b, slot, 2, :, cols], preferred_element_type=F32)
                own[slot, pair] = jnp.where(low_half, both[:CHUNK], both[CHUNK:])
                for sub in range(2):
                    column = slot * 16 + 2 * pair + sub
                    rows = slice(sub * CHUNK, (sub + 1) * CHUNK)
                    packed = jnp.where(lane == column, top[rows], packed)
                    packed = jnp.where(lane == column + 8, total[rows], packed)
        x_both = x_buf[b].reshape(2 * CHUNK, D_MODEL).astype(F32)
        normed = normalize(x_both, gain_ref[...], bias_ref[...])
        up = jnp.dot(normed, wu[...], preferred_element_type=F32) + bu_ref[...]
        hidden = (0.5 * up * (1.0 + lax.erf(up * (0.5 ** 0.5)))).astype(BF16)
        for copy in x_copies(g):
            copy.wait_recv()
        mine = cx_stat[g]
        theirs = pltpu.roll(x_stat[g], 96, 1)
        top = jnp.maximum(jnp.maximum(mine, theirs), packed)
        w_mine = jnp.exp(mine - top)
        w_theirs = jnp.exp(theirs - top)
        w_own = jnp.exp(packed - top)
        total = mine * pltpu.roll(w_mine, 8, 1) + theirs * pltpu.roll(w_theirs, 8, 1) + packed * pltpu.roll(w_own, 8, 1)
        inverse = pltpu.roll(1.0 / jnp.where(is_max, 1.0, total), 120, 1)
        w_mine = w_mine * inverse
        w_theirs = w_theirs * inverse
        w_own = w_own * inverse
        for slot in range(2):
            for pair in range(HEADS // 2):
                cols = slice(pair * PAIR, (pair + 1) * PAIR)
                column = slot * 16 + 2 * pair
                value = o_buf[g, slot, :, cols] * spread(w_mine, column) + x_recv[g, slot, :, cols] * spread(w_theirs, column) + own[slot, pair] * spread(w_own, column)
                ctx[slot * CHUNK:(slot + 1) * CHUNK, cols] = value.astype(BF16)
        branch = jnp.dot(ctx[...], wo[...], preferred_element_type=F32) + jnp.dot(hidden, wd[...], preferred_element_type=F32)
        y_send[g] = branch[CHUNK:]
        y_copy(g).start()
        y_keep[b] = branch[:CHUNK] + x_both[:CHUNK] + bo_ref[...] + bd_ref[...]

    def y_stage(g):
        y_copy(g).wait_recv()
        fin[g, 0] = y_keep[g % 2] + y_recv[g]
        f_copy(g, 0, 2, 0, to_x).start()
        f_copy(g, 0, 1, 1, to_y).start()
        f_copy(g, 0, 4, 2, to_core).start()

    def forward_stage(g):
        f_copy(g, 0, 1, 1, to_y).wait_recv()
        f_copy(g, 0, 2, 0, to_x).wait_recv()

        @pl.when(g % 2 == 0)
        def _():
            f_copy(g, 1, 3, 3, to_x).start()

        @pl.when(g % 2 == 1)
        def _():
            f_copy(g, 2, 3, 3, to_y).start()

        f_copy(g, 1, 5, 4, to_core).start()
        f_copy(g, 2, 6, 5, to_core).start()

    def diagonal_stage(g):
        f_copy(g, 1, 3, 3, to_x).wait_recv()
        f_copy(g, 3, 7, 6, to_core).start()

    def out_stage(g):
        f_copy(g, 0, 4, 2, to_core).wait_recv()
        f_copy(g, 1, 5, 4, to_core).wait_recv()
        f_copy(g, 2, 6, 5, to_core).wait_recv()
        f_copy(g, 3, 7, 6, to_core).wait_recv()

        @pl.when(g >= 2)
        def _():
            for slot in range(GROUP):
                out_copy(g - 2, slot).wait()

        for slot in range(GROUP):
            stage[g % 2, slot] = fin[g, slot].astype(BF16)
            out_copy(g, slot).start()

    for n in range(KV_BUFS - 1):
        for copy in kv_copies(n):
            copy.start()
    for copy in w_copies:
        copy.start()
    barrier = pltpu.get_barrier_semaphore()
    for device in (to_core, to_x, to_y):
        pl.semaphore_signal(barrier, inc=1, device_id=device, device_id_type=pl.DeviceIdType.MESH)
    pl.semaphore_wait(barrier, 3)

    def iteration(i, carry):
        @pl.when(i < GROUPS)
        def _():
            for copy in self_copies(i):
                copy.start()
            stat[i, 0] = jnp.zeros((CHUNK, PAIR), F32)
            stat[i, 1] = jnp.zeros((CHUNK, PAIR), F32)

            def attend_half(half, outer):
                def one(j, inner):
                    attend(i, half * 4 + j)
                    return inner

                lax.fori_loop(0, GROUP // 2, one, 0)

                @pl.when(half == 0)
                def _():
                    for copy in c_copies(i):
                        copy.start()

                return outer

            lax.fori_loop(0, 2, attend_half, 0)
            core_stage(i)

        for depth, work in ((1, x_stage), (2, y_stage), (3, forward_stage), (4, diagonal_stage), (5, out_stage)):
            @pl.when(jnp.logical_and(i >= depth, i < GROUPS + depth))
            def _(depth=depth, work=work):
                if depth == 1:
                    @pl.when(i == 1)
                    def _():
                        for copy in w_copies:
                            copy.wait()

                work(i - depth)

        return carry

    lax.fori_loop(0, GROUPS + 5, iteration, 0)
    for g in (GROUPS - 2, GROUPS - 1):
        for slot in range(GROUP):
            out_copy(g, slot).wait()

    def finish(g, carry):
        for copy in c_copies(g) + x_copies(g) + (y_copy(g),):
            copy.wait_send()
        for src, dst, k, device in ((0, 2, 0, to_x), (0, 1, 1, to_y), (0, 4, 2, to_core), (1, 3, 3, to_x), (1, 5, 4, to_core), (2, 6, 5, to_core), (3, 7, 6, to_core)):
            f_copy(g, src, dst, k, device).wait_send()
        return carry

    lax.fori_loop(0, GROUPS, finish, 0)


def layer_call(lengths, q, kd, vd, k_cache, v_cache, x, gain, bias, w_out, w_up, b_up, w_down, b_out, b_down):
    vmem = pl.BlockSpec(memory_space=pltpu.VMEM)
    dma = pltpu.SemaphoreType.DMA
    return pl.pallas_call(
        layer_kernel,
        in_specs=[pl.BlockSpec(memory_space=pltpu.SMEM), ANY, ANY, ANY, ANY, ANY, ANY, vmem, vmem, ANY, ANY, vmem, ANY, vmem, vmem],
        out_specs=ANY,
        out_shape=jax.ShapeDtypeStruct((ROWS, CHUNK, D_MODEL), BF16),
        scratch_shapes=[
            pltpu.VMEM((WIDTH, D_MODEL), BF16),
            pltpu.VMEM((D_MODEL, FF), BF16),
            pltpu.VMEM((FF, D_MODEL), BF16),
            pltpu.VMEM((KV_BUFS, WIDTH, SLOTS), BF16),
            pltpu.VMEM((KV_BUFS, WIDTH, SLOTS), BF16),
            pltpu.VMEM((KV_BUFS, CHUNK, WIDTH), BF16),
            pltpu.VMEM((2, 2, 3, CHUNK, WIDTH), BF16),
            pltpu.VMEM((2, 2, CHUNK, D_MODEL), BF16),
            pltpu.VMEM((GROUPS, GROUP, CHUNK, WIDTH), F32),
            pltpu.VMEM((GROUPS, 2, CHUNK, PAIR), F32),
            pltpu.VMEM((GROUPS, 4, CHUNK, WIDTH), F32),
            pltpu.VMEM((GROUPS, CHUNK, PAIR), F32),
            pltpu.VMEM((GROUPS, CHUNK, PAIR), F32),
            pltpu.VMEM((GROUPS, 2, CHUNK, WIDTH), F32),
            pltpu.VMEM((GROUPS, CHUNK, PAIR), F32),
            pltpu.VMEM((2 * CHUNK, WIDTH), BF16),
            pltpu.VMEM((GROUPS, CHUNK, D_MODEL), F32),
            pltpu.VMEM((2, CHUNK, D_MODEL), F32),
            pltpu.VMEM((GROUPS, CHUNK, D_MODEL), F32),
            pltpu.VMEM((GROUPS, GROUP, CHUNK, D_MODEL), F32),
            pltpu.VMEM((2, GROUP, CHUNK, D_MODEL), BF16),
            dma((3,)), dma((KV_BUFS, 3)), dma((2, 8)),
            dma((GROUPS, 2)), dma((GROUPS, 2)), dma((GROUPS, 2)), dma((GROUPS, 2)),
            dma((GROUPS,)), dma((GROUPS,)), dma((GROUPS, 7)), dma((GROUPS, GROUP)), dma((2, GROUP)),
        ],
        compiler_params=pltpu.CompilerParams(collective_id=0, has_side_effects=True, vmem_limit_bytes=66_000_000),
        cost_estimate=pl.CostEstimate(flops=30 * 10 ** 9, bytes_accessed=100 << 20, transcendentals=0),
        name="layer",
    )(lengths, q, kd, vd, k_cache, v_cache, x, gain, bias, w_out, w_up, b_up, w_down, b_out, b_down)


def solution(mesh):
    in_specs = (P("dp", None, None), P("dp"), P("dp", "tp", "cp", None), P("dp", "tp", "cp", None), P(), P(), P(), P(), P(None, "tp"), P("tp"), P("tp", None), P(), P(None, "tp"), P("tp"), P("tp", None), P())
    out_specs = (P("dp", None, None), P("dp", "tp", None, None), P("dp", "tp", None, None))
    half = ROT_DIM // 2
    freq = np.broadcast_to((ROPE_BASE ** (-2.0 * np.arange(half) / ROT_DIM)).astype(np.float32)[:, None], (half, 128))

    def local_layer(hidden_in, lengths, k_block, v_block, ln1_gain, ln1_bias, ln2_gain, ln2_bias, w_qkv, b_qkv, w_out, b_out, w_up, b_up, w_down, b_down):
        row = lambda vec: vec.reshape(1, -1).astype(F32)
        b_perm = row(jnp.swapaxes(b_qkv.reshape(HEADS, 3, HEAD_DIM), 0, 1))
        q, k_new, v_new, kd, vd = qkv_call(lengths, hidden_in.reshape(ROWS * CHUNK, D_MODEL), row(ln1_gain), row(ln1_bias), w_qkv, b_perm, jnp.asarray(freq), jnp.asarray(rotate_matrix(), BF16))
        by_row = lambda values: values.reshape(ROWS, CHUNK, WIDTH)
        slot_minor = lambda cache: jnp.swapaxes(cache, 2, 3).reshape(ROWS, WIDTH, SLOTS)
        out = layer_call(lengths, by_row(q), by_row(kd), by_row(vd), slot_minor(k_block), slot_minor(v_block), hidden_in, row(ln2_gain), row(ln2_bias), w_out, w_up, row(b_up), w_down, row(b_out), row(b_down))
        return out, k_new, v_new

    return jax.shard_map(local_layer, mesh=mesh, in_specs=in_specs, out_specs=out_specs, check_vma=False)
```

time: 1140 us -> 198 us (0.17)
  waiting for transfers between devices: 574 us -> 0 us
  matrix products: 235 us -> 0 us
  local copies, waits for them, and re-layouts: 238 us -> 11.3 us
  Pallas kernels: 0 us -> 182 us
  other arithmetic: 68.8 us -> 3.82 us
  between operations: 14.2 us -> 0.64 us
    psum x2 -> x0, waiting for transfers between devices: 543 us -> none  [the longest x1 348 us: local_layer(): branch_sum = lax.psum(attn_part + mlp_part, 'tp')]
    dot_general x6 -> x0, matrix products: 235 us -> none  [the longest x1 93.6 us: local_layer(): jnp.einsum('bcd,df->bcf', normed_mlp, w_up, preferred_element_type=jnp.fl...]
    pallas_call x0 -> x2, Pallas kernels: none -> 182 us  [the longest x1 149 us: layer_call(): pl.pallas_call(layer_kernel, in_specs=[pl.BlockSpec(memory_space=pltpu.SM...]
    unnamed x42 -> x1, local copies, waits for them, and re-layouts: 89.1 us -> 8.58 us
    slice x3 -> x0, local copies, waits for them, and re-layouts: 65.9 us -> none  [the longest x1 53.9 us: local_layer(): v_chunk = qkv_all[:, :, :, 2]]
    reshape x1 -> x0, local copies, waits for them, and re-layouts: 62.6 us -> none  [local_layer(): qkv_all = qkv_all.reshape(num_rows, chunk_len, heads_here, 3, head_dim)]
    reduce_sum x3 -> x0, other arithmetic: 31.9 us -> none  [the longest x1 21.6 us: cache_piece(): return (piece_max, probs.sum(axis=-1), piece_out)]
    pmax x1 -> x0, waiting for transfers between devices: 31.1 us -> none  [local_layer(): global_max = lax.pmax(jnp.maximum(cache_max, own_max), 'cp')]
  transfers between devices with their start and end apart: 3 -> 0, of which waited for: 3 -> 0; matrix products, arithmetic and copies ran while one was open for 12% -> 0% of each run, Pallas kernels for 0% -> 0%
where the time goes in v1:
time: 198 us
  Pallas kernels  182 us (92%)
  local copies, waits for them, and re-layouts  11.3 us (6%)
  other arithmetic  3.82 us (2%)
    pallas_call x1, Pallas kernels, layer_call(): pl.pallas_call(layer_kernel, in_specs=[pl.BlockSpec(memory_space=pltpu.SM...  149 us
    pallas_call x1, Pallas kernels, qkv_call(): pl.pallas_call(qkv_kernel, grid=(steps,), in_specs=[pl.BlockSpec(memory_s...  32.8 us
    unnamed x1, local copies, waits for them, and re-layouts  8.58 us

profile of v1, /device:TPU:1, one launch (start us, length us, event | category | flops | bytes accessed | tf_op | source)
XLA Modules:
  0.0 197.8 jit_solution(14799086502816745135)
XLA Ops:
  0.6 1.3 convert_element_type.36
  1.9 1.3 convert_element_type.37
  3.2 1.3 convert_element_type.35
  4.5 0.8 reshape.77
  5.2 0.7 reshape.73.bq_ref
  5.9 1.3 jit_solution_.3.freq_ref
  7.2 32.8 %qkv.1 = (bf16[4096,512]{1,0:T(8,128)(2,1)}, bf16[64,8,64,64]{3,2,1,0:T(8,128)(2,1)}, bf16[64,8,64,64]{3,2,1,0:T(8,128)(2,1)}, bf16[4096,512]{1,0:T(8,128)(2,1)}, bf16[4096,512]{1,0:T(8,128)(2,1)}) custom-call(s32[64]{0:T(128)} %len_ref.3, bf16[4096,1024]{1,0:T(8,128)(2,1)} %bitcast.24, f32[1,1024]{1,0:T(1,128)} %bitcast.25, f32[1,1024]{1,0:T(1,128)} %bitcast.26, ...), custom_call_target="tpu_custom_call" | custom-call | flops 12884901888 | bytes 41943040 | tf_op jit(solution)/shard_map/qkv/pallas_call | solution.py:112
  40.0 149.1 %layer.1 = bf16[64,64,1024]{2,1,0:T(8,128)(2,1)} custom-call(s32[64]{0:T(128)} %len_ref.3, bf16[64,64,512]{2,1,0:T(8,128)(2,1)} %bitcast.29, bf16[64,64,512]{2,1,0:T(8,128)(2,1)} %bitcast.30, bf16[64,64,512]{2,1,0:T(8,128)(2,1)} %bitcast.31, bf16[64,512,512]{2,1,0:T(8,128)(2,1)} %bitcast.22, bf16[64,512,512]{2,1,0:T(8,128)(2,1)} %bitcast.23, ...), custom_call_target="tpu_custom_call" | custom-call | flops 30000001024 | bytes 104857600 | tf_op jit(solution)/shard_map/layer/pallas_call | solution.py:407
  189.2 8.6 %copy.23 = bf16[64,64,1024]{2,1,0:T(8,128)(2,1)} copy(bf16[64,64,1024]{2,1,0:T(8,128)(2,1)} %layer.1) | data formatting | bytes 16777216
  (1 shorter events, 0.0 us)

commit v2 on v1

v2 whole, which is shorter than its diff:
```python
import functools
import numpy as np
import jax
import jax.numpy as jnp
from jax import lax
from jax.experimental import pallas as pl
from jax.experimental.pallas import tpu as pltpu
from jax.sharding import PartitionSpec as P

EPSILON = 1e-5
NEG_BIG = -1e30
MAX_FLOOR = -1e29
ROPE_BASE = 10000.0
HEAD_DIM = 64
ROT_DIM = 16
PAIR = 2 * HEAD_DIM
ROWS = 64
CHUNK = 64
HEADS = 8
WIDTH = HEADS * HEAD_DIM
SLOTS = 512
D_MODEL = 1024
FF = 2048
GROUP = 8
GROUPS = ROWS // GROUP
KV_BUFS = 3
QUAD = 4 * HEAD_DIM
HALF = GROUP // 2
TAIL_ROWS = 4
TAIL_TOKENS = TAIL_ROWS * CHUNK
F32 = jnp.float32
BF16 = jnp.bfloat16
ANY = pl.BlockSpec(memory_space=pl.ANY)


def normalize(x_f32, gain, bias):
    row_mean = jnp.mean(x_f32, axis=-1, keepdims=True)
    centered = x_f32 - row_mean
    variance = jnp.mean(centered * centered, axis=-1, keepdims=True)
    return (centered * lax.rsqrt(variance + EPSILON) * gain + bias).astype(BF16)


def rotate_matrix():
    matrix = np.zeros((PAIR, PAIR), np.float32)
    half = ROT_DIM // 2
    for base in (0, HEAD_DIM):
        for i in range(half):
            matrix[base + half + i, base + i] = -1.0
            matrix[base + i, base + half + i] = 1.0
    return matrix


def swap_halves(pair):
    return jnp.concatenate([pair[:, HEAD_DIM:], pair[:, :HEAD_DIM]], axis=1)


def pick_parts(blocks, low_half):
    first, second, third = blocks
    return jnp.where(low_half, first, second), swap_halves(jnp.where(low_half, third, first)), jnp.where(low_half, second, third)


def bias_parts(bias_row):
    low_half = lax.broadcasted_iota(jnp.int32, (1, PAIR), 1) < HEAD_DIM
    parts = [pick_parts([bias_row[:, (3 * pair + k) * PAIR:(3 * pair + k + 1) * PAIR] for k in range(3)], low_half) for pair in range(HEADS // 2)]
    return [jnp.concatenate([parts[pair][k] for pair in range(HEADS // 2)], axis=1) for k in range(3)]


def row_tables(trig, row):
    cos_len = trig[0, pl.ds(row, 1), :]
    sin_len = trig[1, pl.ds(row, 1), :]
    cos_c = trig[2]
    sin_c = trig[3]
    return cos_len * cos_c - sin_len * sin_c, sin_len * cos_c + cos_len * sin_c


def tail_kernel(a_ref, w_ref, bq_ref, trig_ref, rot_ref, through_ref, out_ref, k_out, v_out):
    step = pl.program_id(0)
    out_ref[...] = through_ref[...]
    _, k_bias, v_bias = bias_parts(bq_ref[...].astype(F32).reshape(1, 3 * WIDTH))
    k_all = (jnp.dot(a_ref[...], w_ref[:, :WIDTH], preferred_element_type=F32) + k_bias).astype(BF16)
    v_all = (jnp.dot(a_ref[...], w_ref[:, WIDTH:], preferred_element_type=F32) + v_bias).astype(BF16)
    tables = [row_tables(trig_ref, step * TAIL_ROWS + row) for row in range(TAIL_ROWS)]
    cos_tab = jnp.concatenate([table[0] for table in tables], axis=0)
    sin_tab = jnp.concatenate([table[1] for table in tables], axis=0)
    for pair in range(HEADS // 2):
        cols = slice(pair * PAIR, (pair + 1) * PAIR)
        x = k_all[:, cols]
        turned = jnp.dot(x, rot_ref[...], preferred_element_type=F32)
        k_pair = (x.astype(F32) * cos_tab + turned * sin_tab).astype(BF16)
        v_pair = v_all[:, cols]
        for row in range(TAIL_ROWS):
            tokens = slice(row * CHUNK, (row + 1) * CHUNK)
            for sub in range(2):
                dims = slice(sub * HEAD_DIM, (sub + 1) * HEAD_DIM)
                k_out[row, 2 * pair + sub] = k_pair[tokens, dims]
                v_out[row, 2 * pair + sub] = v_pair[tokens, dims]


def tail_call(a_flat, w_kv, b_qkv, trig, rot, through):
    tokens = ROWS * CHUNK
    whole = lambda shape: pl.BlockSpec(shape, lambda i: (0,) * len(shape))
    dense = pl.BlockSpec((TAIL_TOKENS, D_MODEL), lambda i: (i, 0))
    heads = pl.BlockSpec((TAIL_ROWS, HEADS, CHUNK, HEAD_DIM), lambda i: (i, 0, 0, 0))
    return pl.pallas_call(
        tail_kernel,
        grid=(ROWS // TAIL_ROWS,),
        in_specs=[dense, whole((D_MODEL, 2 * WIDTH)), whole((3 * WIDTH,)), whole((4, CHUNK, PAIR)), whole((PAIR, PAIR)), dense],
        out_specs=[dense, heads, heads],
        out_shape=[
            jax.ShapeDtypeStruct((tokens, D_MODEL), BF16),
            jax.ShapeDtypeStruct((ROWS, HEADS, CHUNK, HEAD_DIM), BF16),
            jax.ShapeDtypeStruct((ROWS, HEADS, CHUNK, HEAD_DIM), BF16),
        ],
        cost_estimate=pl.CostEstimate(flops=2 * tokens * D_MODEL * 2 * WIDTH, bytes_accessed=42 << 20, transcendentals=0),
        name="tail",
    )(a_flat, w_kv, b_qkv, trig, rot, through)


def layer_kernel(len_ref, kc_hbm, vc_hbm, x_hbm, gain1_ref, bias1_ref, gain2_ref, bias2_ref, wqkv_hbm, bq_ref, rot_ref, wo_hbm, wu_hbm, bu_ref, wd_hbm, bo_ref, bd_ref,
                 out_hbm, a_hbm, wkv_hbm, trig_hbm,
                 wo, wu, wd, wq, wkv, bias_q, bias_kv, trig, kbuf, vbuf, x_buf, a_buf, q_buf, kv_self, own_o, own_stat, mlp_acc,
                 o_buf, stat, c_recv, c_stat, cx_stat, x_recv, x_stat, ctx, y_send, y_keep, y_recv, fin, stage,
                 w_sem, kv_sem, xin_sem, a_sem, side_sem, c_ssem, c_rsem, x_ssem, x_rsem, y_ssem, y_rsem, f_ssem, f_rsem, out_sem):
    tp_id = lax.axis_index("tp")
    cp_id = lax.axis_index("cp")
    chip_x = cp_id // 2
    core = cp_id % 2
    to_core = {"cp": 2 * chip_x + 1 - core}
    to_x = {"cp": 2 * (1 - chip_x) + core}
    to_y = {"tp": 1 - tp_id}

    def flip(bit, mine):
        return bit + mine - 2 * bit * mine

    def row_of(group, slot):
        return group * GROUP + 4 * flip(slot // 4, core) + 2 * flip((slot // 2) % 2, chip_x) + flip(slot % 2, tp_id)

    def remote(src, dst, ssem, rsem, device):
        return pltpu.make_async_remote_copy(src_ref=src, dst_ref=dst, send_sem=ssem, recv_sem=rsem, device_id=device, device_id_type=pl.DeviceIdType.MESH)

    def kv_copies(n):
        b = n % KV_BUFS
        row = row_of(n // GROUP, (n % GROUP + 4) % GROUP)
        return (pltpu.make_async_copy(kc_hbm.at[row], kbuf.at[b], kv_sem.at[b, 0]), pltpu.make_async_copy(vc_hbm.at[row], vbuf.at[b], kv_sem.at[b, 1]))

    def x_in(g):
        return [pltpu.make_async_copy(x_hbm.at[row_of(g, slot)], x_buf.at[g % 2, slot], xin_sem.at[g % 2, slot]) for slot in range(GROUP)]

    def a_copies(g, half):
        first = 4 - 4 * half
        return [pltpu.make_async_copy(a_buf.at[half, pl.ds(k * CHUNK, CHUNK)], a_hbm.at[row_of(g, first + k)], a_sem.at[half, k]) for k in range(HALF)]

    wqkv_copy = pltpu.make_async_copy(wqkv_hbm, wu.at[:, pl.ds(0, 3 * WIDTH)], w_sem.at[0])
    w_copies = [pltpu.make_async_copy(wu_hbm, wu, w_sem.at[1]), pltpu.make_async_copy(wd_hbm, wd, w_sem.at[2])]
    for head in range(HEADS):
        w_copies.append(pltpu.make_async_copy(wo_hbm.at[pl.ds(head * HEAD_DIM, HEAD_DIM)], wo.at[pl.ds((head % 2) * QUAD + (head // 2) * HEAD_DIM, HEAD_DIM)], w_sem.at[3 + head]))
    side_copies = (pltpu.make_async_copy(wkv, wkv_hbm, side_sem.at[0]), pltpu.make_async_copy(trig, trig_hbm, side_sem.at[1]))

    def c_copies(g):
        return (remote(o_buf.at[g, pl.ds(4, 4)], c_recv.at[g], c_ssem.at[g, 0], c_rsem.at[g, 0], to_core), remote(stat.at[g, 0], c_stat.at[g], c_ssem.at[g, 1], c_rsem.at[g, 1], to_core))

    def x_copies(g):
        return (remote(o_buf.at[g, pl.ds(2, 2)], x_recv.at[g], x_ssem.at[g, 0], x_rsem.at[g, 0], to_x), remote(cx_stat.at[g, pl.ds(2, 2)], x_stat.at[g], x_ssem.at[g, 1], x_rsem.at[g, 1], to_x))

    def y_copy(g):
        return remote(y_send.at[g], y_recv.at[g], y_ssem.at[g], y_rsem.at[g], to_y)

    def f_copy(g, src, dst, k, device):
        return remote(fin.at[g, src], fin.at[g, dst], f_ssem.at[g, k], f_rsem.at[g, dst], device)

    def out_copy(g, slot):
        return pltpu.make_async_copy(stage.at[g % 2, slot], out_hbm.at[row_of(g, slot)], out_sem.at[g % 2, slot])

    lane = lax.broadcasted_iota(jnp.int32, (CHUNK, PAIR), 1)
    low_half = lane < HEAD_DIM
    is_max = lax.broadcasted_iota(jnp.int32, (8, PAIR), 0) < HEADS // 2
    quad_lane = lax.broadcasted_iota(jnp.int32, (CHUNK, QUAD), 1)

    def block_diagonal(q_quad):
        zero = jnp.zeros_like(q_quad)
        return jnp.concatenate([jnp.where(quad_lane // HEAD_DIM == k, q_quad, zero) for k in range(4)], axis=0)

    def rotate(values, turned, tables, scale):
        return ((values.astype(F32) * tables[0] + turned * tables[1]) * scale).astype(BF16)

    def project(g, half):
        first = 4 - 4 * half

        @pl.when(g >= 1)
        def _():
            for copy in a_copies(g - 1, half):
                copy.wait()

        x = x_buf[g % 2, first:first + HALF].reshape(HALF * CHUNK, D_MODEL).astype(F32)
        normed = normalize(x, gain1_ref[...].reshape(1, D_MODEL), bias1_ref[...].reshape(1, D_MODEL))
        a_buf[half] = normed
        for copy in a_copies(g, half):
            copy.start()
        q_all = (jnp.dot(normed, wq[...], preferred_element_type=F32) + bias_q[...]).astype(BF16)
        tables = [row_tables(trig, row_of(g, first + k)) for k in range(HALF)]
        for pair in range(HEADS // 2):
            cols = slice(pair * PAIR, (pair + 1) * PAIR)
            turned = jnp.dot(q_all[:, cols], rot_ref[...], preferred_element_type=F32)
            for k in range(HALF):
                tokens = slice(k * CHUNK, (k + 1) * CHUNK)
                q_buf[first + k, :, cols] = rotate(q_all[tokens, cols], turned[tokens], tables[k], HEAD_DIM ** -0.5)

    def attend(g, half, j):
        n = g * GROUP + half * HALF + j
        slot = 4 - 4 * half + j
        b = n % KV_BUFS
        for copy in kv_copies(n):
            copy.wait()

        @pl.when(n + KV_BUFS - 1 < ROWS)
        def _():
            for copy in kv_copies(n + KV_BUFS - 1):
                copy.start()

        row_len = len_ref[row_of(g, slot)]
        valid = cp_id * SLOTS + lax.broadcasted_iota(jnp.int32, (SLOTS, QUAD), 0) < row_len
        for quad in range(2):
            dims = slice(quad * QUAD, (quad + 1) * QUAD)
            q4 = block_diagonal(q_buf[slot, :, dims])
            scores = lax.dot_general(kbuf[b, dims, :], q4, (((0,), (1,)), ((), ())), preferred_element_type=F32)
            scores = jnp.where(valid, scores, NEG_BIG)
            top = jnp.maximum(jnp.max(scores, axis=0, keepdims=True), MAX_FLOOR)
            probs = jnp.exp(scores - top)
            total = jnp.sum(probs, axis=0, keepdims=True)
            packed = probs.astype(BF16)
            for sub in range(2):
                pair = 2 * quad + sub
                cols = slice(sub * PAIR, (sub + 1) * PAIR)
                both = jnp.dot(vbuf[b, pair * PAIR:(pair + 1) * PAIR, :], packed[:, cols], preferred_element_type=F32)
                o_buf[g, slot, pair * HEAD_DIM:(pair + 1) * HEAD_DIM, :] = jnp.where(low_half, both[:HEAD_DIM], both[HEAD_DIM:])
                stat[g, half, j, pair:pair + 1, :] = top[:, cols]
                stat[g, half, j, 4 + pair:5 + pair, :] = total[:, cols]

    def core_stage(g):
        for copy in c_copies(g):
            copy.wait_recv()
        for slot in (2, 3, 0, 1):
            mine = stat[g, 1, slot]
            theirs = c_stat[g, slot]
            top = jnp.maximum(mine, theirs)
            w_mine = jnp.exp(mine - top)
            w_theirs = jnp.exp(theirs - top)
            total = mine * pltpu.roll(w_mine, 4, 0) + theirs * pltpu.roll(w_theirs, 4, 0)
            cx_stat[g, slot] = jnp.where(is_max, top, total)
            for pair in range(HEADS // 2):
                dims = slice(pair * HEAD_DIM, (pair + 1) * HEAD_DIM)
                o_buf[g, slot, dims, :] = o_buf[g, slot, dims, :] * w_mine[pair:pair + 1] + c_recv[g, slot, dims, :] * w_theirs[pair:pair + 1]
            if slot == 3:
                for copy in x_copies(g):
                    copy.start()

    def prepare(g):
        kv = (jnp.dot(a_buf[1, :2 * CHUNK], wkv[...], preferred_element_type=F32) + bias_kv[...]).astype(BF16)
        tables = [row_tables(trig, row_of(g, slot)) for slot in range(2)]
        for pair in range(HEADS // 2):
            cols = slice(pair * PAIR, (pair + 1) * PAIR)
            turned = jnp.dot(kv[:, cols], rot_ref[...], preferred_element_type=F32)
            for slot in range(2):
                tokens = slice(slot * CHUNK, (slot + 1) * CHUNK)
                kv_self[slot, :, cols] = rotate(kv[tokens, cols], turned[tokens], tables[slot], 1.0)
        for slot in range(2):
            kv_self[slot, :, WIDTH:] = kv[slot * CHUNK:(slot + 1) * CHUNK, WIDTH:]
        causal = lax.broadcasted_iota(jnp.int32, (CHUNK, QUAD), 0) <= quad_lane % CHUNK
        for slot in range(2):
            for quad in range(2):
                dims = slice(quad * QUAD, (quad + 1) * QUAD)
                q4 = block_diagonal(q_buf[slot, :, dims])
                scores = lax.dot_general(kv_self[slot, :, dims], q4, (((1,), (1,)), ((), ())), preferred_element_type=F32)
                scores = jnp.where(causal, scores, NEG_BIG)
                top = jnp.max(scores, axis=0, keepdims=True)
                probs = jnp.where(causal, jnp.exp(scores - top), 0.0)
                total = jnp.sum(probs, axis=0, keepdims=True)
                packed = probs.astype(BF16)
                for sub in range(2):
                    pair = 2 * quad + sub
                    cols = slice(sub * PAIR, (sub + 1) * PAIR)
                    both = lax.dot_general(kv_self[slot, :, WIDTH + pair * PAIR:WIDTH + (pair + 1) * PAIR], packed[:, cols], (((0,), (0,)), ((), ())), preferred_element_type=F32)
                    own_o[slot, pair * HEAD_DIM:(pair + 1) * HEAD_DIM, :] = jnp.where(low_half, both[:HEAD_DIM], both[HEAD_DIM:])
                    own_stat[slot, pair:pair + 1, :] = top[:, cols]
                    own_stat[slot, 4 + pair:5 + pair, :] = total[:, cols]
        x_both = x_buf[g % 2, :2].reshape(2 * CHUNK, D_MODEL).astype(F32)
        normed = normalize(x_both, gain2_ref[...].reshape(1, D_MODEL), bias2_ref[...].reshape(1, D_MODEL))
        up = jnp.dot(normed, wu[...], preferred_element_type=F32) + bu_ref[...].astype(F32).reshape(1, FF)
        hidden = (0.5 * up * (1.0 + lax.erf(up * (0.5 ** 0.5)))).astype(BF16)
        mlp_acc[...] = jnp.dot(hidden, wd[...], preferred_element_type=F32)
        y_keep[g % 2] = x_both[:CHUNK] + bo_ref[...].astype(F32).reshape(1, D_MODEL) + bd_ref[...].astype(F32).reshape(1, D_MODEL)

    def x_stage(g):
        for copy in x_copies(g):
            copy.wait_recv()
        for slot in range(2):
            mine = cx_stat[g, slot]
            theirs = x_stat[g, slot]
            own = own_stat[slot]
            top = jnp.maximum(jnp.maximum(mine, theirs), own)
            w_mine = jnp.exp(mine - top)
            w_theirs = jnp.exp(theirs - top)
            w_own = jnp.exp(own - top)
            total = mine * pltpu.roll(w_mine, 4, 0) + theirs * pltpu.roll(w_theirs, 4, 0) + own * pltpu.roll(w_own, 4, 0)
            inverse = pltpu.roll(1.0 / jnp.where(is_max, 1.0, total), 4, 0)
            w_mine = w_mine * inverse
            w_theirs = w_theirs * inverse
            w_own = w_own * inverse
            values = []
            for pair in range(HEADS // 2):
                dims = slice(pair * HEAD_DIM, (pair + 1) * HEAD_DIM)
                one = slice(pair, pair + 1)
                values.append(o_buf[g, slot, dims, :] * w_mine[one] + x_recv[g, slot, dims, :] * w_theirs[one] + own_o[slot, dims, :] * w_own[one])
            turned = jnp.concatenate(values, axis=0).T
            for half in range(2):
                ctx[slot * CHUNK:(slot + 1) * CHUNK, half * QUAD:(half + 1) * QUAD] = turned[half * CHUNK:(half + 1) * CHUNK].astype(BF16)
        branch = jnp.dot(ctx[...], wo[...], preferred_element_type=F32) + mlp_acc[...]
        y_send[g] = branch[CHUNK:]
        y_copy(g).start()
        y_keep[g % 2] = y_keep[g % 2] + branch[:CHUNK]

    def y_stage(g):
        y_copy(g).wait_recv()
        fin[g, 0] = y_keep[g % 2] + y_recv[g]
        f_copy(g, 0, 2, 0, to_x).start()
        f_copy(g, 0, 1, 1, to_y).start()
        f_copy(g, 0, 4, 2, to_core).start()

    def forward_stage(g):
        f_copy(g, 0, 1, 1, to_y).wait_recv()
        f_copy(g, 0, 2, 0, to_x).wait_recv()

        @pl.when(g % 2 == 0)
        def _():
            f_copy(g, 1, 3, 3, to_x).start()

        @pl.when(g % 2 == 1)
        def _():
            f_copy(g, 2, 3, 3, to_y).start()

        f_copy(g, 1, 5, 4, to_core).start()
        f_copy(g, 2, 6, 5, to_core).start()

    def diagonal_stage(g):
        f_copy(g, 1, 3, 3, to_x).wait_recv()
        f_copy(g, 3, 7, 6, to_core).start()

    def out_stage(g):
        f_copy(g, 0, 4, 2, to_core).wait_recv()
        f_copy(g, 1, 5, 4, to_core).wait_recv()
        f_copy(g, 2, 6, 5, to_core).wait_recv()
        f_copy(g, 3, 7, 6, to_core).wait_recv()

        @pl.when(g >= 2)
        def _():
            for slot in range(GROUP):
                out_copy(g - 2, slot).wait()

        for slot in range(GROUP):
            stage[g % 2, slot] = fin[g, slot].astype(BF16)
            out_copy(g, slot).start()

    def when_group(g, work):
        @pl.when(jnp.logical_and(g >= 0, g < GROUPS))
        def _():
            work(g)

    wqkv_copy.start()
    for copy in x_in(0):
        copy.start()
    for n in range(KV_BUFS - 1):
        for copy in kv_copies(n):
            copy.start()
    barrier = pltpu.get_barrier_semaphore()
    for device in (to_core, to_x, to_y):
        pl.semaphore_signal(barrier, inc=1, device_id=device, device_id_type=pl.DeviceIdType.MESH)

    dim = lane % HEAD_DIM
    freq = jnp.zeros((CHUNK, PAIR), F32)
    for k in range(ROT_DIM // 2):
        here = jnp.logical_and(dim % (ROT_DIM // 2) == k, dim < ROT_DIM)
        freq = jnp.where(here, float(np.float32(ROPE_BASE ** (-2.0 * k / ROT_DIM))), freq)

    def one_angle(r, carry):
        trig[0, pl.ds(r, 1), :] = len_ref[r].astype(F32) * freq[:1]
        return carry

    lax.fori_loop(0, ROWS, one_angle, 0)
    angles = trig[0]
    trig[1] = jnp.sin(angles)
    trig[0] = jnp.cos(angles)
    angles = lax.broadcasted_iota(jnp.int32, (CHUNK, PAIR), 0).astype(F32) * freq
    trig[2] = jnp.cos(angles)
    trig[3] = jnp.sin(angles)
    q_bias, k_bias, v_bias = bias_parts(bq_ref[...].astype(F32).reshape(1, 3 * WIDTH))
    bias_q[...] = q_bias
    bias_kv[:, :WIDTH] = k_bias
    bias_kv[:, WIDTH:] = v_bias
    wqkv_copy.wait()

    def arrange(r, carry):
        rows = pl.ds(pl.multiple_of(r * PAIR, PAIR), PAIR)
        low = lax.broadcasted_iota(jnp.int32, (PAIR, PAIR), 1) < HEAD_DIM
        for pair in range(HEADS // 2):
            q_part, k_part, v_part = pick_parts([wu[rows, (3 * pair + k) * PAIR:(3 * pair + k + 1) * PAIR] for k in range(3)], low)
            wq[rows, pair * PAIR:(pair + 1) * PAIR] = q_part
            wkv[rows, pair * PAIR:(pair + 1) * PAIR] = k_part
            wkv[rows, WIDTH + pair * PAIR:WIDTH + (pair + 1) * PAIR] = v_part
        return carry

    lax.fori_loop(0, D_MODEL // PAIR, arrange, 0)
    for copy in w_copies:
        copy.start()
    for copy in side_copies:
        copy.start()
    pl.semaphore_wait(barrier, 3)

    def iteration(i, carry):
        @pl.when(i + 1 < GROUPS)
        def _():
            for copy in x_in(i + 1):
                copy.start()

        for half in range(2):
            @pl.when(i < GROUPS)
            def _(half=half):
                if half == 0:
                    for copy in x_in(i):
                        copy.wait()
                project(i, half)
                lax.fori_loop(0, HALF, lambda j, inner: (attend(i, half, j), inner)[1], 0)
                if half == 0:
                    for copy in c_copies(i):
                        copy.start()
                else:
                    core_stage(i)

            if half == 0:
                when_group(i - 1, x_stage)
                when_group(i - 2, forward_stage)

        @pl.when(i == 0)
        def _():
            for copy in w_copies:
                copy.wait()

        when_group(i, prepare)
        when_group(i - 1, y_stage)
        when_group(i - 2, diagonal_stage)
        when_group(i - 3, out_stage)
        return carry

    lax.fori_loop(0, GROUPS + 3, iteration, 0)
    for copy in side_copies:
        copy.wait()
    for half in range(2):
        for copy in a_copies(GROUPS - 1, half):
            copy.wait()
    for g in (GROUPS - 2, GROUPS - 1):
        for slot in range(GROUP):
            out_copy(g, slot).wait()

    def finish(g, carry):
        for copy in c_copies(g) + x_copies(g) + (y_copy(g),):
            copy.wait_send()
        for src, dst, k, device in ((0, 2, 0, to_x), (0, 1, 1, to_y), (0, 4, 2, to_core), (1, 3, 3, to_x), (1, 5, 4, to_core), (2, 6, 5, to_core), (3, 7, 6, to_core)):
            f_copy(g, src, dst, k, device).wait_send()
        return carry

    lax.fori_loop(0, GROUPS, finish, 0)


def layer_call(lengths, k_cache, v_cache, x, gain1, bias1, gain2, bias2, w_qkv, b_qkv, rot, w_out, w_up, b_up, w_down, b_out, b_down):
    vmem = pl.BlockSpec(memory_space=pltpu.VMEM)
    dma = pltpu.SemaphoreType.DMA
    return pl.pallas_call(
        layer_kernel,
        in_specs=[pl.BlockSpec(memory_space=pltpu.SMEM), ANY, ANY, ANY, vmem, vmem, vmem, vmem, ANY, vmem, vmem, ANY, ANY, vmem, ANY, vmem, vmem],
        out_specs=[ANY, ANY, ANY, ANY],
        out_shape=[
            jax.ShapeDtypeStruct((ROWS, CHUNK, D_MODEL), BF16),
            jax.ShapeDtypeStruct((ROWS, CHUNK, D_MODEL), BF16),
            jax.ShapeDtypeStruct((D_MODEL, 2 * WIDTH), BF16),
            jax.ShapeDtypeStruct((4, CHUNK, PAIR), F32),
        ],
        scratch_shapes=[
            pltpu.VMEM((WIDTH, D_MODEL), BF16),
            pltpu.VMEM((D_MODEL, FF), BF16),
            pltpu.VMEM((FF, D_MODEL), BF16),
            pltpu.VMEM((D_MODEL, WIDTH), BF16),
            pltpu.VMEM((D_MODEL, 2 * WIDTH), BF16),
            pltpu.VMEM((1, WIDTH), F32),
            pltpu.VMEM((1, 2 * WIDTH), F32),
            pltpu.VMEM((4, CHUNK, PAIR), F32),
            pltpu.VMEM((KV_BUFS, WIDTH, SLOTS), BF16),
            pltpu.VMEM((KV_BUFS, WIDTH, SLOTS), BF16),
            pltpu.VMEM((2, GROUP, CHUNK, D_MODEL), BF16),
            pltpu.VMEM((2, HALF * CHUNK, D_MODEL), BF16),
            pltpu.VMEM((GROUP, CHUNK, WIDTH), BF16),
            pltpu.VMEM((2, CHUNK, 2 * WIDTH), BF16),
            pltpu.VMEM((2, QUAD, PAIR), F32),
            pltpu.VMEM((2, 8, PAIR), F32),
            pltpu.VMEM((2 * CHUNK, D_MODEL), F32),
            pltpu.VMEM((GROUPS, GROUP, QUAD, PAIR), F32),
            pltpu.VMEM((GROUPS, 2, HALF, 8, PAIR), F32),
            pltpu.VMEM((GROUPS, HALF, QUAD, PAIR), F32),
            pltpu.VMEM((GROUPS, HALF, 8, PAIR), F32),
            pltpu.VMEM((GROUPS, HALF, 8, PAIR), F32),
            pltpu.VMEM((GROUPS, 2, QUAD, PAIR), F32),
            pltpu.VMEM((GROUPS, 2, 8, PAIR), F32),
            pltpu.VMEM((2 * CHUNK, WIDTH), BF16),
            pltpu.VMEM((GROUPS, CHUNK, D_MODEL), F32),
            pltpu.VMEM((2, CHUNK, D_MODEL), F32),
            pltpu.VMEM((GROUPS, CHUNK, D_MODEL), F32),
            pltpu.VMEM((GROUPS, GROUP, CHUNK, D_MODEL), F32),
            pltpu.VMEM((2, GROUP, CHUNK, D_MODEL), BF16),
            dma((3 + HEADS,)), dma((KV_BUFS, 2)), dma((2, GROUP)), dma((2, HALF)), dma((2,)),
            dma((GROUPS, 2)), dma((GROUPS, 2)), dma((GROUPS, 2)), dma((GROUPS, 2)),
            dma((GROUPS,)), dma((GROUPS,)), dma((GROUPS, 7)), dma((GROUPS, GROUP)), dma((2, GROUP)),
        ],
        compiler_params=pltpu.CompilerParams(collective_id=0, has_side_effects=True, vmem_limit_bytes=67_000_000),
        cost_estimate=pl.CostEstimate(flops=30 * 10 ** 9, bytes_accessed=100 << 20, transcendentals=0),
        name="layer",
    )(lengths, k_cache, v_cache, x, gain1, bias1, gain2, bias2, w_qkv, b_qkv, rot, w_out, w_up, b_up, w_down, b_out, b_down)


def solution(mesh):
    in_specs = (P("dp", None, None), P("dp"), P("dp", "tp", "cp", None), P("dp", "tp", "cp", None), P(), P(), P(), P(), P(None, "tp"), P("tp"), P("tp", None), P(), P(None, "tp"), P("tp"), P("tp", None), P())
    out_specs = (P("dp", None, None), P("dp", "tp", None, None), P("dp", "tp", None, None))

    def local_layer(hidden_in, lengths, k_block, v_block, ln1_gain, ln1_bias, ln2_gain, ln2_bias, w_qkv, b_qkv, w_out, b_out, w_up, b_up, w_down, b_down):
        slot_minor = lambda cache: jnp.swapaxes(cache, 2, 3).reshape(ROWS, WIDTH, SLOTS)
        rot = jnp.asarray(rotate_matrix(), BF16)
        through, normed, w_kv, trig = layer_call(lengths, slot_minor(k_block), slot_minor(v_block), hidden_in, ln1_gain, ln1_bias, ln2_gain, ln2_bias, w_qkv, b_qkv, rot, w_out, w_up, b_up, w_down, b_out, b_down)
        flat = lambda values: values.reshape(ROWS * CHUNK, D_MODEL)
        out, k_new, v_new = tail_call(flat(normed), w_kv, b_qkv, trig, rot, flat(through))
        return out.reshape(ROWS, CHUNK, D_MODEL), k_new, v_new

    return jax.shard_map(local_layer, mesh=mesh, in_specs=in_specs, out_specs=out_specs, check_vma=False)
```

time: 198 us -> 201 us (1.015)
  Pallas kernels: 182 us -> 199 us
  local copies, waits for them, and re-layouts: 11.3 us -> 0 us
  other arithmetic: 3.82 us -> 0 us
    pallas_call x1, Pallas kernels: 149 us -> 174 us  [layer_call(): pl.pallas_call(layer_kernel, in_specs=[pl.BlockSpec(memory_space=pltpu.SM...]
    unnamed x1 -> x0, local copies, waits for them, and re-layouts: 8.58 us -> none
    pallas_call x1, Pallas kernels: 32.8 us -> 25 us  [tail_call(): pl.pallas_call(tail_kernel, grid=(ROWS // TAIL_ROWS,), in_specs=[dense, w...]
    convert_element_type x3 -> x0, other arithmetic: 3.82 us -> none  [local_layer(): row = lambda vec: vec.reshape(1, -1).astype(F32)]
where the time goes in v2:
time: 201 us; the launch traced here: 199 us
  Pallas kernels  199 us (99%)
    pallas_call x1, Pallas kernels, layer_call(): pl.pallas_call(layer_kernel, in_specs=[pl.BlockSpec(memory_space=pltpu.SM...  174 us
    pallas_call x1, Pallas kernels, tail_call(): pl.pallas_call(tail_kernel, grid=(ROWS // TAIL_ROWS,), in_specs=[dense, w...  25 us

profile of v2, /device:TPU:1, one launch (start us, length us, event | category | flops | bytes accessed | tf_op | source)
XLA Modules:
  0.0 199.2 jit_solution(8752768151220424536)
XLA Ops:
  0.6 173.6 %layer.1 = (bf16[64,64,1024]{2,1,0:T(8,128)(2,1)}, bf16[64,64,1024]{2,1,0:T(8,128)(2,1)}, bf16[1024,1024]{1,0:T(8,128)(2,1)}, f32[4,64,128]{2,1,0:T(8,128)}) custom-call(s32[64]{0:T(128)} %len_ref.1, bf16[64,512,512]{2,1,0:T(8,128)(2,1)} %bitcast.9, bf16[64,512,512]{2,1,0:T(8,128)(2,1)} %bitcast.10, bf16[64,64,1024]{2,1,0:T(8,128)(2,1)} %x_hbm.1, ...), custom_call_target="tpu_custom_call" | custom-call | flops 30000001024 | bytes 104857600 | tf_op jit(solution)/shard_map/layer/pallas_call | solution.py:476
  174.2 25.0 %tail.1 = (bf16[4096,1024]{1,0:T(8,128)(2,1)}, bf16[64,8,64,64]{3,2,1,0:T(8,128)(2,1)}, bf16[64,8,64,64]{3,2,1,0:T(8,128)(2,1)}) custom-call(bf16[4096,1024]{1,0:T(8,128)(2,1)} %bitcast.13, bf16[1024,1024]{1,0:T(8,128)(2,1)} %get-tuple-element.11.w_ref, bf16[1536]{0:T(1024)(128)(2,1)} %bq_ref.3, f32[4,64,128]{2,1,0:T(8,128)} %get-tuple-element.12.trig_ref, ...), custom_call_target="tpu_custom_call" | custom-call | flops 8589934592 | bytes 44040192 | tf_op jit(solution)/shard_map/tail/pallas_call | solution.py:104

commit v3 on v2

--- a/solution.py
+++ b/solution.py
@@ -23,11 +23,18 @@
 FF = 2048
 GROUP = 8
 GROUPS = ROWS // GROUP
-KV_BUFS = 3
+K_BUFS = 3
+V_BUFS = 5
+AHEAD = 2
+STRIP = 64
+FORWARD_LAG = 5
+DIAGONAL_LAG = 8
 QUAD = 4 * HEAD_DIM
 HALF = GROUP // 2
-TAIL_ROWS = 4
+TAIL_ROWS = 16
 TAIL_TOKENS = TAIL_ROWS * CHUNK
+TAIL_SLOTS = 2
+PASS_STEPS = 2
 F32 = jnp.float32
 BF16 = jnp.bfloat16
 ANY = pl.BlockSpec(memory_space=pl.ANY)
@@ -73,54 +80,122 @@
     return cos_len * cos_c - sin_len * sin_c, sin_len * cos_c + cos_len * sin_c
 
 
-def tail_kernel(a_ref, w_ref, bq_ref, trig_ref, rot_ref, through_ref, out_ref, k_out, v_out):
-    step = pl.program_id(0)
-    out_ref[...] = through_ref[...]
+def tail_kernel(a_hbm, w_hbm, bq_ref, trig_ref, rot_ref, through_hbm, out_hbm, k_hbm, v_hbm, w_ref, a_all, passing, raw, bias, k_stage, v_stage, w_sem, a_sem, in_sem, out_sem, k_sem, v_sem):
+    blocks = ROWS // TAIL_ROWS
+
+    def tokens(i):
+        return pl.ds(i * TAIL_TOKENS, TAIL_TOKENS)
+
+    def rows(i):
+        return pl.ds(i * TAIL_ROWS, TAIL_ROWS)
+
+    w_copy = pltpu.make_async_copy(w_hbm, w_ref, w_sem)
+    a_in = lambda i: pltpu.make_async_copy(a_hbm.at[tokens(i)], a_all.at[i], a_sem.at[i])
+    pass_in = lambda i: pltpu.make_async_copy(through_hbm.at[tokens(i)], passing.at[i], in_sem.at[i])
+    pass_out = lambda i: pltpu.make_async_copy(passing.at[i], out_hbm.at[tokens(i)], out_sem.at[i])
+    k_put = lambda i: pltpu.make_async_copy(k_stage.at[i % TAIL_SLOTS], k_hbm.at[rows(i)], k_sem.at[i % TAIL_SLOTS])
+    v_put = lambda i: pltpu.make_async_copy(v_stage.at[i % TAIL_SLOTS], v_hbm.at[rows(i)], v_sem.at[i % TAIL_SLOTS])
+
+    w_copy.start()
+    for i in range(blocks):
+        a_in(i).start()
+        if i >= 2:
+            pass_in(i - 2).start()
+    for i in range(blocks - 2, blocks):
+        pass_in(i).start()
     _, k_bias, v_bias = bias_parts(bq_ref[...].astype(F32).reshape(1, 3 * WIDTH))
-    k_all = (jnp.dot(a_ref[...], w_ref[:, :WIDTH], preferred_element_type=F32) + k_bias).astype(BF16)
-    v_all = (jnp.dot(a_ref[...], w_ref[:, WIDTH:], preferred_element_type=F32) + v_bias).astype(BF16)
-    tables = [row_tables(trig_ref, step * TAIL_ROWS + row) for row in range(TAIL_ROWS)]
-    cos_tab = jnp.concatenate([table[0] for table in tables], axis=0)
-    sin_tab = jnp.concatenate([table[1] for table in tables], axis=0)
-    for pair in range(HEADS // 2):
-        cols = slice(pair * PAIR, (pair + 1) * PAIR)
-        x = k_all[:, cols]
-        turned = jnp.dot(x, rot_ref[...], preferred_element_type=F32)
-        k_pair = (x.astype(F32) * cos_tab + turned * sin_tab).astype(BF16)
-        v_pair = v_all[:, cols]
+    bias[:, :WIDTH] = k_bias
+    bias[:, WIDTH:] = v_bias
+    w_copy.wait()
+
+    def multiply(i):
+        raw[...] = (jnp.dot(a_all[i], w_ref[...], preferred_element_type=F32) + bias[...]).astype(BF16)
+
+    def place(i):
+        slot = i % TAIL_SLOTS
         for row in range(TAIL_ROWS):
-            tokens = slice(row * CHUNK, (row + 1) * CHUNK)
-            for sub in range(2):
-                dims = slice(sub * HEAD_DIM, (sub + 1) * HEAD_DIM)
-                k_out[row, 2 * pair + sub] = k_pair[tokens, dims]
-                v_out[row, 2 * pair + sub] = v_pair[tokens, dims]
+            tables = row_tables(trig_ref, i * TAIL_ROWS + row)
+            here = slice(row * CHUNK, (row + 1) * CHUNK)
+            for pair in range(HEADS // 2):
+                x = raw[here, pair * PAIR:(pair + 1) * PAIR]
+                turned = jnp.dot(x, rot_ref[...], preferred_element_type=F32)
+                k_pair = (x.astype(F32) * tables[0] + turned * tables[1]).astype(BF16)
+                v_pair = raw[here, WIDTH + pair * PAIR:WIDTH + (pair + 1) * PAIR]
+                for sub in range(2):
+                    dims = slice(sub * HEAD_DIM, (sub + 1) * HEAD_DIM)
+                    k_stage[slot, row, 2 * pair + sub] = k_pair[:, dims]
+                    v_stage[slot, row, 2 * pair + sub] = v_pair[:, dims]
+
+    def step(i, carry):
+        @pl.when(i < blocks)
+        def _():
+            a_in(i).wait()
+
+        @pl.when(i >= 1 + TAIL_SLOTS)
+        def _():
+            k_put(i - 1 - TAIL_SLOTS).wait()
+            v_put(i - 1 - TAIL_SLOTS).wait()
+
+        place(jnp.maximum(i - 1, 0))
+        multiply(jnp.minimum(i, blocks - 1))
+
+        @pl.when(i >= 1)
+        def _():
+            k_put(i - 1).start()
+            v_put(i - 1).start()
+
+        for early in range(PASS_STEPS):
+            @pl.when(i == early + 1)
+            def _(early=early):
+                for block in range(early * blocks // PASS_STEPS, (early + 1) * blocks // PASS_STEPS):
+                    pass_in(block).wait()
+                    pass_out(block).start()
+
+        return carry
+
+    lax.fori_loop(0, blocks + 1, step, 0)
+    for i in range(blocks - TAIL_SLOTS, blocks):
+        k_put(i).wait()
+        v_put(i).wait()
+    for i in range(blocks):
+        pass_out(i).wait()
 
 
 def tail_call(a_flat, w_kv, b_qkv, trig, rot, through):
     tokens = ROWS * CHUNK
-    whole = lambda shape: pl.BlockSpec(shape, lambda i: (0,) * len(shape))
-    dense = pl.BlockSpec((TAIL_TOKENS, D_MODEL), lambda i: (i, 0))
-    heads = pl.BlockSpec((TAIL_ROWS, HEADS, CHUNK, HEAD_DIM), lambda i: (i, 0, 0, 0))
+    blocks = ROWS // TAIL_ROWS
+    vmem = pl.BlockSpec(memory_space=pltpu.VMEM)
+    dma = pltpu.SemaphoreType.DMA
     return pl.pallas_call(
         tail_kernel,
-        grid=(ROWS // TAIL_ROWS,),
-        in_specs=[dense, whole((D_MODEL, 2 * WIDTH)), whole((3 * WIDTH,)), whole((4, CHUNK, PAIR)), whole((PAIR, PAIR)), dense],
-        out_specs=[dense, heads, heads],
+        in_specs=[ANY, ANY, vmem, vmem, vmem, ANY],
+        out_specs=[ANY, ANY, ANY],
         out_shape=[
             jax.ShapeDtypeStruct((tokens, D_MODEL), BF16),
             jax.ShapeDtypeStruct((ROWS, HEADS, CHUNK, HEAD_DIM), BF16),
             jax.ShapeDtypeStruct((ROWS, HEADS, CHUNK, HEAD_DIM), BF16),
         ],
+        scratch_shapes=[
+            pltpu.VMEM((D_MODEL, 2 * WIDTH), BF16),
+            pltpu.VMEM((blocks, TAIL_TOKENS, D_MODEL), BF16),
+            pltpu.VMEM((blocks, TAIL_TOKENS, D_MODEL), BF16),
+            pltpu.VMEM((TAIL_TOKENS, 2 * WIDTH), BF16),
+            pltpu.VMEM((1, 2 * WIDTH), F32),
+            pltpu.VMEM((TAIL_SLOTS, TAIL_ROWS, HEADS, CHUNK, HEAD_DIM), BF16),
+            pltpu.VMEM((TAIL_SLOTS, TAIL_ROWS, HEADS, CHUNK, HEAD_DIM), BF16),
+            dma(()), dma((blocks,)), dma((blocks,)), dma((blocks,)), dma((TAIL_SLOTS,)), dma((TAIL_SLOTS,)),
+        ],
         cost_estimate=pl.CostEstimate(flops=2 * tokens * D_MODEL * 2 * WIDTH, bytes_accessed=42 << 20, transcendentals=0),
+        compiler_params=pltpu.CompilerParams(vmem_limit_bytes=60_000_000),
         name="tail",
     )(a_flat, w_kv, b_qkv, trig, rot, through)
 
 
 def layer_kernel(len_ref, kc_hbm, vc_hbm, x_hbm, gain1_ref, bias1_ref, gain2_ref, bias2_ref, wqkv_hbm, bq_ref, rot_ref, wo_hbm, wu_hbm, bu_ref, wd_hbm, bo_ref, bd_ref,
                  out_hbm, a_hbm, wkv_hbm, trig_hbm,
-                 wo, wu, wd, wq, wkv, bias_q, bias_kv, trig, kbuf, vbuf, x_buf, a_buf, q_buf, kv_self, own_o, own_stat, mlp_acc,
+                 wo, wu, wd, wq, wkv, bias_q, bias_kv, trig, kbuf, vbuf, s0, s1, p0, p1, x_buf, a_buf, q_buf, kv_self, own_o, own_stat, mlp_acc,
                  o_buf, stat, c_recv, c_stat, cx_stat, x_recv, x_stat, ctx, y_send, y_keep, y_recv, fin, stage,
-                 w_sem, kv_sem, xin_sem, a_sem, side_sem, c_ssem, c_rsem, x_ssem, x_rsem, y_ssem, y_rsem, f_ssem, f_rsem, out_sem):
+                 w_sem, k_sem, v_sem, xin_sem, a_sem, side_sem, c_ssem, c_rsem, x_ssem, x_rsem, y_ssem, y_rsem, f_ssem, f_rsem, out_sem):
     tp_id = lax.axis_index("tp")
     cp_id = lax.axis_index("cp")
     chip_x = cp_id // 2
@@ -139,9 +214,10 @@
         return pltpu.make_async_remote_copy(src_ref=src, dst_ref=dst, send_sem=ssem, recv_sem=rsem, device_id=device, device_id_type=pl.DeviceIdType.MESH)
 
     def kv_copies(n):
-        b = n % KV_BUFS
+        kb = n % K_BUFS
+        vb = n % V_BUFS
         row = row_of(n // GROUP, (n % GROUP + 4) % GROUP)
-        return (pltpu.make_async_copy(kc_hbm.at[row], kbuf.at[b], kv_sem.at[b, 0]), pltpu.make_async_copy(vc_hbm.at[row], vbuf.at[b], kv_sem.at[b, 1]))
+        return (pltpu.make_async_copy(kc_hbm.at[row], kbuf.at[kb], k_sem.at[kb]), pltpu.make_async_copy(vc_hbm.at[row], vbuf.at[vb], v_sem.at[vb]))
 
     def x_in(g):
         return [pltpu.make_async_copy(x_hbm.at[row_of(g, slot)], x_buf.at[g % 2, slot], xin_sem.at[g % 2, slot]) for slot in range(GROUP)]
@@ -205,36 +281,90 @@
                 tokens = slice(k * CHUNK, (k + 1) * CHUNK)
                 q_buf[first + k, :, cols] = rotate(q_all[tokens, cols], turned[tokens], tables[k], HEAD_DIM ** -0.5)
 
-    def attend(g, half, j):
-        n = g * GROUP + half * HALF + j
-        slot = 4 - 4 * half + j
-        b = n % KV_BUFS
-        for copy in kv_copies(n):
-            copy.wait()
-
-        @pl.when(n + KV_BUFS - 1 < ROWS)
-        def _():
-            for copy in kv_copies(n + KV_BUFS - 1):
-                copy.start()
-
+    def slot_at(j):
+        return (j + HALF) % GROUP
+
+    def score_unit(g, j, quad, s_buf):
+        slot = slot_at(j)
+        dims = slice(quad * QUAD, (quad + 1) * QUAD)
         row_len = len_ref[row_of(g, slot)]
         valid = cp_id * SLOTS + lax.broadcasted_iota(jnp.int32, (SLOTS, QUAD), 0) < row_len
-        for quad in range(2):
-            dims = slice(quad * QUAD, (quad + 1) * QUAD)
-            q4 = block_diagonal(q_buf[slot, :, dims])
-            scores = lax.dot_general(kbuf[b, dims, :], q4, (((0,), (1,)), ((), ())), preferred_element_type=F32)
-            scores = jnp.where(valid, scores, NEG_BIG)
-            top = jnp.maximum(jnp.max(scores, axis=0, keepdims=True), MAX_FLOOR)
-            probs = jnp.exp(scores - top)
-            total = jnp.sum(probs, axis=0, keepdims=True)
-            packed = probs.astype(BF16)
-            for sub in range(2):
-                pair = 2 * quad + sub
-                cols = slice(sub * PAIR, (sub + 1) * PAIR)
-                both = jnp.dot(vbuf[b, pair * PAIR:(pair + 1) * PAIR, :], packed[:, cols], preferred_element_type=F32)
-                o_buf[g, slot, pair * HEAD_DIM:(pair + 1) * HEAD_DIM, :] = jnp.where(low_half, both[:HEAD_DIM], both[HEAD_DIM:])
-                stat[g, half, j, pair:pair + 1, :] = top[:, cols]
-                stat[g, half, j, 4 + pair:5 + pair, :] = total[:, cols]
+        q4 = block_diagonal(q_buf[slot, :, dims])
+        scores = lax.dot_general(kbuf[(g * GROUP + j) % K_BUFS, dims, :], q4, (((0,), (1,)), ((), ())), preferred_element_type=F32)
+        s_buf[...] = jnp.where(valid, scores, NEG_BIG)
+
+    def soft_unit(g, j, quad, s_buf, p_buf):
+        top = jnp.full((8, QUAD), MAX_FLOOR, F32)
+        for k in range(SLOTS // STRIP):
+            top = jnp.maximum(top, jnp.max(s_buf[k * STRIP:(k + 1) * STRIP, :].reshape(STRIP // 8, 8, QUAD), axis=0))
+        top = jnp.max(top, axis=0, keepdims=True)
+        total = jnp.zeros((8, QUAD), F32)
+        for k in range(SLOTS // STRIP):
+            slots = slice(k * STRIP, (k + 1) * STRIP)
+            probs = jnp.exp(s_buf[slots, :] - top)
+            total = total + jnp.sum(probs.reshape(STRIP // 8, 8, QUAD), axis=0)
+            p_buf[slots, :] = probs.astype(BF16)
+        total = jnp.sum(total, axis=0, keepdims=True)
+        for sub in range(2):
+            pair = 2 * quad + sub
+            cols = slice(sub * PAIR, (sub + 1) * PAIR)
+            stat[g, j // HALF, j % HALF, pair:pair + 1, :] = top[:, cols]
+            stat[g, j // HALF, j % HALF, 4 + pair:5 + pair, :] = total[:, cols]
+
+    def value_unit(g, j, quad, p_buf):
+        slot = slot_at(j)
+        for sub in range(2):
+            pair = 2 * quad + sub
+            both = jnp.dot(vbuf[(g * GROUP + j) % V_BUFS, pair * PAIR:(pair + 1) * PAIR, :], p_buf[:, sub * PAIR:(sub + 1) * PAIR], preferred_element_type=F32)
+            o_buf[g, slot, pair * HEAD_DIM:(pair + 1) * HEAD_DIM, :] = jnp.where(low_half, both[:HEAD_DIM], both[HEAD_DIM:])
+
+    def attend_group(g):
+        first = g * GROUP
+
+        def fetch(j):
+            for copy in kv_copies(first + j):
+                copy.wait()
+
+            @pl.when(first + j + AHEAD < ROWS)
+            def _():
+                for copy in kv_copies(first + j + AHEAD):
+                    copy.start()
+
+        def scores_of(j):
+            score_unit(g, j, 0, s0)
+            score_unit(g, j, 1, s1)
+
+        def soft_of(j):
+            soft_unit(g, j, 0, s0, p0)
+            soft_unit(g, j, 1, s1, p1)
+
+        def values_of(j):
+            value_unit(g, j, 0, p0)
+            value_unit(g, j, 1, p1)
+
+        fetch(0)
+        scores_of(0)
+        fetch(1)
+        soft_of(0)
+        scores_of(1)
+
+        def step(j, carry):
+            fetch(j)
+            values_of(j - 2)
+            soft_of(j - 1)
+            scores_of(j)
+
+            @pl.when(j == HALF + 1)
+            def _():
+                for copy in c_copies(g):
+                    copy.start()
+
+            return carry
+
+        lax.fori_loop(2, GROUP, step, 0)
+        values_of(GROUP - 2)
+        soft_of(GROUP - 1)
+        values_of(GROUP - 1)
 
     def core_stage(g):
         for copy in c_copies(g):
@@ -288,7 +418,7 @@
         up = jnp.dot(normed, wu[...], preferred_element_type=F32) + bu_ref[...].astype(F32).reshape(1, FF)
         hidden = (0.5 * up * (1.0 + lax.erf(up * (0.5 ** 0.5)))).astype(BF16)
         mlp_acc[...] = jnp.dot(hidden, wd[...], preferred_element_type=F32)
-        y_keep[g % 2] = x_both[:CHUNK] + bo_ref[...].astype(F32).reshape(1, D_MODEL) + bd_ref[...].astype(F32).reshape(1, D_MODEL)
+        y_keep[g % 3] = x_both[:CHUNK] + bo_ref[...].astype(F32).reshape(1, D_MODEL) + bd_ref[...].astype(F32).reshape(1, D_MODEL)
 
     def x_stage(g):
         for copy in x_copies(g):
@@ -317,11 +447,11 @@
         branch = jnp.dot(ctx[...], wo[...], preferred_element_type=F32) + mlp_acc[...]
         y_send[g] = branch[CHUNK:]
         y_copy(g).start()
-        y_keep[g % 2] = y_keep[g % 2] + branch[:CHUNK]
+        y_keep[g % 3] = y_keep[g % 3] + branch[:CHUNK]
 
     def y_stage(g):
         y_copy(g).wait_recv()
-        fin[g, 0] = y_keep[g % 2] + y_recv[g]
+        fin[g, 0] = y_keep[g % 3] + y_recv[g]
         f_copy(g, 0, 2, 0, to_x).start()
         f_copy(g, 0, 1, 1, to_y).start()
         f_copy(g, 0, 4, 2, to_core).start()
@@ -368,7 +498,7 @@
     wqkv_copy.start()
     for copy in x_in(0):
         copy.start()
-    for n in range(KV_BUFS - 1):
+    for n in range(AHEAD):
         for copy in kv_copies(n):
             copy.start()
     barrier = pltpu.get_barrier_semaphore()
@@ -421,23 +551,21 @@
             for copy in x_in(i + 1):
                 copy.start()
 
-        for half in range(2):
-            @pl.when(i < GROUPS)
-            def _(half=half):
-                if half == 0:
-                    for copy in x_in(i):
-                        copy.wait()
-                project(i, half)
-                lax.fori_loop(0, HALF, lambda j, inner: (attend(i, half, j), inner)[1], 0)
-                if half == 0:
-                    for copy in c_copies(i):
-                        copy.start()
-                else:
-                    core_stage(i)
-
-            if half == 0:
-                when_group(i - 1, x_stage)
-                when_group(i - 2, forward_stage)
+        when_group(i - DIAGONAL_LAG, diagonal_stage)
+
+        @pl.when(i < GROUPS)
+        def _():
+            for copy in x_in(i):
+                copy.wait()
+            project(i, 0)
+            project(i, 1)
+            attend_group(i)
+            core_stage(i)
+
+        when_group(i - 1, x_stage)
+        when_group(i - FORWARD_LAG, forward_stage)
+        when_group(i - DIAGONAL_LAG, out_stage)
+        when_group(i - 2, y_stage)
 
         @pl.when(i == 0)
         def _():
@@ -445,12 +573,9 @@
                 copy.wait()
 
         when_group(i, prepare)
-        when_group(i - 1, y_stage)
-        when_group(i - 2, diagonal_stage)
-        when_group(i - 3, out_stage)
         return carry
 
-    lax.fori_loop(0, GROUPS + 3, iteration, 0)
+    lax.fori_loop(0, GROUPS + DIAGONAL_LAG, iteration, 0)
     for copy in side_copies:
         copy.wait()
     for half in range(2):
@@ -492,8 +617,12 @@
             pltpu.VMEM((1, WIDTH), F32),
             pltpu.VMEM((1, 2 * WIDTH), F32),
             pltpu.VMEM((4, CHUNK, PAIR), F32),
-            pltpu.VMEM((KV_BUFS, WIDTH, SLOTS), BF16),
-            pltpu.VMEM((KV_BUFS, WIDTH, SLOTS), BF16),
+            pltpu.VMEM((K_BUFS, WIDTH, SLOTS), BF16),
+            pltpu.VMEM((V_BUFS, WIDTH, SLOTS), BF16),
+            pltpu.VMEM((SLOTS, QUAD), F32),
+            pltpu.VMEM((SLOTS, QUAD), F32),
+            pltpu.VMEM((SLOTS, QUAD), BF16),
+            pltpu.VMEM((SLOTS, QUAD), BF16),
             pltpu.VMEM((2, GROUP, CHUNK, D_MODEL), BF16),
             pltpu.VMEM((2, HALF * CHUNK, D_MODEL), BF16),
             pltpu.VMEM((GROUP, CHUNK, WIDTH), BF16),
@@ -510,11 +639,11 @@
             pltpu.VMEM((GROUPS, 2, 8, PAIR), F32),
             pltpu.VMEM((2 * CHUNK, WIDTH), BF16),
             pltpu.VMEM((GROUPS, CHUNK, D_MODEL), F32),
-            pltpu.VMEM((2, CHUNK, D_MODEL), F32),
+            pltpu.VMEM((3, CHUNK, D_MODEL), F32),
             pltpu.VMEM((GROUPS, CHUNK, D_MODEL), F32),
             pltpu.VMEM((GROUPS, GROUP, CHUNK, D_MODEL), F32),
             pltpu.VMEM((2, GROUP, CHUNK, D_MODEL), BF16),
-            dma((3 + HEADS,)), dma((KV_BUFS, 2)), dma((2, GROUP)), dma((2, HALF)), dma((2,)),
+            dma((3 + HEADS,)), dma((K_BUFS,)), dma((V_BUFS,)), dma((2, GROUP)), dma((2, HALF)), dma((2,)),
             dma((GROUPS, 2)), dma((GROUPS, 2)), dma((GROUPS, 2)), dma((GROUPS, 2)),
             dma((GROUPS,)), dma((GROUPS,)), dma((GROUPS, 7)), dma((GROUPS, GROUP)), dma((2, GROUP)),
         ],

time: 201 us -> 175 us (0.87)
  Pallas kernels: 199 us -> 173 us
    pallas_call x1, Pallas kernels: 174 us -> 151 us  [layer_call(): pl.pallas_call(layer_kernel, in_specs=[pl.BlockSpec(memory_space=pltpu.SM...]
    pallas_call x1, Pallas kernels: 25 us -> 22.5 us  [tail_call(): pl.pallas_call(tail_kernel, in_specs=[ANY, ANY, vmem, vmem, vmem, ANY], o...]
where the time goes in v3:
time: 175 us; the launch traced here: 174 us
  Pallas kernels  173 us (99%)
    pallas_call x1, Pallas kernels, layer_call(): pl.pallas_call(layer_kernel, in_specs=[pl.BlockSpec(memory_space=pltpu.SM...  151 us
    pallas_call x1, Pallas kernels, tail_call(): pl.pallas_call(tail_kernel, in_specs=[ANY, ANY, vmem, vmem, vmem, ANY], o...  22.5 us

profile of v3, /device:TPU:1, one launch (start us, length us, event | category | flops | bytes accessed | tf_op | source)
XLA Modules:
  0.0 173.9 jit_solution(2489099120011593942)
XLA Ops:
  0.6 150.8 %layer.1 = (bf16[64,64,1024]{2,1,0:T(8,128)(2,1)}, bf16[64,64,1024]{2,1,0:T(8,128)(2,1)}, bf16[1024,1024]{1,0:T(8,128)(2,1)}, f32[4,64,128]{2,1,0:T(8,128)}) custom-call(s32[64]{0:T(128)} %len_ref.1, bf16[64,512,512]{2,1,0:T(8,128)(2,1)} %bitcast.9, bf16[64,512,512]{2,1,0:T(8,128)(2,1)} %bitcast.10, bf16[64,64,1024]{2,1,0:T(8,128)(2,1)} %x_hbm.1, ...), custom_call_target="tpu_custom_call" | custom-call | flops 30000001024 | bytes 104857600 | tf_op jit(solution)/shard_map/layer/pallas_call | solution.py:601
  151.5 22.5 %tail.1 = (bf16[4096,1024]{1,0:T(8,128)(2,1)}, bf16[64,8,64,64]{3,2,1,0:T(8,128)(2,1)}, bf16[64,8,64,64]{3,2,1,0:T(8,128)(2,1)}) custom-call(bf16[4096,1024]{1,0:T(8,128)(2,1)} %bitcast.13, bf16[1024,1024]{1,0:T(8,128)(2,1)} %get-tuple-element.11.w_hbm, bf16[1536]{0:T(1024)(128)(2,1)} %bq_ref.3, f32[4,64,128]{2,1,0:T(8,128)} %get-tuple-element.12.trig_ref, ...), custom_call_target="tpu_custom_call" | custom-call | flops 8589934592 | bytes 44040192 | tf_op jit(solution)/shard_map/tail/pallas_call | solution.py:169

commit v4 on v3

--- a/solution.py
+++ b/solution.py
@@ -29,12 +29,11 @@
 STRIP = 64
 FORWARD_LAG = 5
 DIAGONAL_LAG = 8
+OUT_LAG = 9
 QUAD = 4 * HEAD_DIM
 HALF = GROUP // 2
-TAIL_ROWS = 16
-TAIL_TOKENS = TAIL_ROWS * CHUNK
-TAIL_SLOTS = 2
-PASS_STEPS = 2
+TAIL_ROWS = 4
+TAIL_SLOTS = 4
 F32 = jnp.float32
 BF16 = jnp.bfloat16
 ANY = pl.BlockSpec(memory_space=pl.ANY)
@@ -80,80 +79,42 @@
     return cos_len * cos_c - sin_len * sin_c, sin_len * cos_c + cos_len * sin_c
 
 
-def tail_kernel(a_hbm, w_hbm, bq_ref, trig_ref, rot_ref, through_hbm, out_hbm, k_hbm, v_hbm, w_ref, a_all, passing, raw, bias, k_stage, v_stage, w_sem, a_sem, in_sem, out_sem, k_sem, v_sem):
+def tail_kernel(kv_hbm, through_hbm, out_hbm, k_hbm, v_hbm, kv_all, passing, k_stage, v_stage, kv_sem, in_sem, out_sem, k_sem, v_sem):
     blocks = ROWS // TAIL_ROWS
-
-    def tokens(i):
-        return pl.ds(i * TAIL_TOKENS, TAIL_TOKENS)
 
     def rows(i):
         return pl.ds(i * TAIL_ROWS, TAIL_ROWS)
 
-    w_copy = pltpu.make_async_copy(w_hbm, w_ref, w_sem)
-    a_in = lambda i: pltpu.make_async_copy(a_hbm.at[tokens(i)], a_all.at[i], a_sem.at[i])
-    pass_in = lambda i: pltpu.make_async_copy(through_hbm.at[tokens(i)], passing.at[i], in_sem.at[i])
-    pass_out = lambda i: pltpu.make_async_copy(passing.at[i], out_hbm.at[tokens(i)], out_sem.at[i])
+    kv_in = lambda i: pltpu.make_async_copy(kv_hbm.at[rows(i)], kv_all.at[i], kv_sem.at[i])
+    pass_in = lambda i: pltpu.make_async_copy(through_hbm.at[rows(i)], passing.at[i], in_sem.at[i])
+    pass_out = lambda i: pltpu.make_async_copy(passing.at[i], out_hbm.at[rows(i)], out_sem.at[i])
     k_put = lambda i: pltpu.make_async_copy(k_stage.at[i % TAIL_SLOTS], k_hbm.at[rows(i)], k_sem.at[i % TAIL_SLOTS])
     v_put = lambda i: pltpu.make_async_copy(v_stage.at[i % TAIL_SLOTS], v_hbm.at[rows(i)], v_sem.at[i % TAIL_SLOTS])
 
-    w_copy.start()
     for i in range(blocks):
-        a_in(i).start()
-        if i >= 2:
-            pass_in(i - 2).start()
-    for i in range(blocks - 2, blocks):
+        kv_in(i).start()
         pass_in(i).start()
-    _, k_bias, v_bias = bias_parts(bq_ref[...].astype(F32).reshape(1, 3 * WIDTH))
-    bias[:, :WIDTH] = k_bias
-    bias[:, WIDTH:] = v_bias
-    w_copy.wait()
-
-    def multiply(i):
-        raw[...] = (jnp.dot(a_all[i], w_ref[...], preferred_element_type=F32) + bias[...]).astype(BF16)
-
-    def place(i):
+
+    def step(i, carry):
+        @pl.when(i >= TAIL_SLOTS)
+        def _():
+            k_put(i - TAIL_SLOTS).wait()
+            v_put(i - TAIL_SLOTS).wait()
+
+        kv_in(i).wait()
         slot = i % TAIL_SLOTS
         for row in range(TAIL_ROWS):
-            tables = row_tables(trig_ref, i * TAIL_ROWS + row)
-            here = slice(row * CHUNK, (row + 1) * CHUNK)
-            for pair in range(HEADS // 2):
-                x = raw[here, pair * PAIR:(pair + 1) * PAIR]
-                turned = jnp.dot(x, rot_ref[...], preferred_element_type=F32)
-                k_pair = (x.astype(F32) * tables[0] + turned * tables[1]).astype(BF16)
-                v_pair = raw[here, WIDTH + pair * PAIR:WIDTH + (pair + 1) * PAIR]
-                for sub in range(2):
-                    dims = slice(sub * HEAD_DIM, (sub + 1) * HEAD_DIM)
-                    k_stage[slot, row, 2 * pair + sub] = k_pair[:, dims]
-                    v_stage[slot, row, 2 * pair + sub] = v_pair[:, dims]
-
-    def step(i, carry):
-        @pl.when(i < blocks)
-        def _():
-            a_in(i).wait()
-
-        @pl.when(i >= 1 + TAIL_SLOTS)
-        def _():
-            k_put(i - 1 - TAIL_SLOTS).wait()
-            v_put(i - 1 - TAIL_SLOTS).wait()
-
-        place(jnp.maximum(i - 1, 0))
-        multiply(jnp.minimum(i, blocks - 1))
-
-        @pl.when(i >= 1)
-        def _():
-            k_put(i - 1).start()
-            v_put(i - 1).start()
-
-        for early in range(PASS_STEPS):
-            @pl.when(i == early + 1)
-            def _(early=early):
-                for block in range(early * blocks // PASS_STEPS, (early + 1) * blocks // PASS_STEPS):
-                    pass_in(block).wait()
-                    pass_out(block).start()
-
+            for head in range(HEADS):
+                dims = slice(head * HEAD_DIM, (head + 1) * HEAD_DIM)
+                k_stage[slot, row, head] = kv_all[i, row, :, dims]
+                v_stage[slot, row, head] = kv_all[i, row, :, WIDTH + head * HEAD_DIM:WIDTH + (head + 1) * HEAD_DIM]
+        k_put(i).start()
+        v_put(i).start()
+        pass_in(i).wait()
+        pass_out(i).start()
         return carry
 
-    lax.fori_loop(0, blocks + 1, step, 0)
+    lax.fori_loop(0, blocks, step, 0)
     for i in range(blocks - TAIL_SLOTS, blocks):
         k_put(i).wait()
         v_put(i).wait()
@@ -161,41 +122,36 @@
         pass_out(i).wait()
 
 
-def tail_call(a_flat, w_kv, b_qkv, trig, rot, through):
-    tokens = ROWS * CHUNK
+def tail_call(kv, through):
     blocks = ROWS // TAIL_ROWS
-    vmem = pl.BlockSpec(memory_space=pltpu.VMEM)
     dma = pltpu.SemaphoreType.DMA
     return pl.pallas_call(
         tail_kernel,
-        in_specs=[ANY, ANY, vmem, vmem, vmem, ANY],
+        in_specs=[ANY, ANY],
         out_specs=[ANY, ANY, ANY],
         out_shape=[
-            jax.ShapeDtypeStruct((tokens, D_MODEL), BF16),
+            jax.ShapeDtypeStruct((ROWS, CHUNK, D_MODEL), BF16),
             jax.ShapeDtypeStruct((ROWS, HEADS, CHUNK, HEAD_DIM), BF16),
             jax.ShapeDtypeStruct((ROWS, HEADS, CHUNK, HEAD_DIM), BF16),
         ],
         scratch_shapes=[
-            pltpu.VMEM((D_MODEL, 2 * WIDTH), BF16),
-            pltpu.VMEM((blocks, TAIL_TOKENS, D_MODEL), BF16),
-            pltpu.VMEM((blocks, TAIL_TOKENS, D_MODEL), BF16),
-            pltpu.VMEM((TAIL_TOKENS, 2 * WIDTH), BF16),
-            pltpu.VMEM((1, 2 * WIDTH), F32),
+            pltpu.VMEM((blocks, TAIL_ROWS, CHUNK, D_MODEL), BF16),
+            pltpu.VMEM((blocks, TAIL_ROWS, CHUNK, D_MODEL), BF16),
             pltpu.VMEM((TAIL_SLOTS, TAIL_ROWS, HEADS, CHUNK, HEAD_DIM), BF16),
             pltpu.VMEM((TAIL_SLOTS, TAIL_ROWS, HEADS, CHUNK, HEAD_DIM), BF16),
-            dma(()), dma((blocks,)), dma((blocks,)), dma((blocks,)), dma((TAIL_SLOTS,)), dma((TAIL_SLOTS,)),
+            dma((blocks,)), dma((blocks,)), dma((blocks,)), dma((TAIL_SLOTS,)), dma((TAIL_SLOTS,)),
         ],
-        cost_estimate=pl.CostEstimate(flops=2 * tokens * D_MODEL * 2 * WIDTH, bytes_accessed=42 << 20, transcendentals=0),
+        cost_estimate=pl.CostEstimate(flops=1 << 20, bytes_accessed=42 << 20, transcendentals=0),
         compiler_params=pltpu.CompilerParams(vmem_limit_bytes=60_000_000),
         name="tail",
-    )(a_flat, w_kv, b_qkv, trig, rot, through)
+    )(kv, through)
 
 
 def layer_kernel(len_ref, kc_hbm, vc_hbm, x_hbm, gain1_ref, bias1_ref, gain2_ref, bias2_ref, wqkv_hbm, bq_ref, rot_ref, wo_hbm, wu_hbm, bu_ref, wd_hbm, bo_ref, bd_ref,
-                 out_hbm, a_hbm, wkv_hbm, trig_hbm,
+                 out_hbm, a_hbm, kv_hbm,
                  wo, wu, wd, wq, wkv, bias_q, bias_kv, trig, kbuf, vbuf, s0, s1, p0, p1, x_buf, a_buf, q_buf, kv_self, own_o, own_stat, mlp_acc,
                  o_buf, stat, c_recv, c_stat, cx_stat, x_recv, x_stat, ctx, y_send, y_keep, y_recv, fin, stage,
-                 w_sem, k_sem, v_sem, xin_sem, a_sem, side_sem, c_ssem, c_rsem, x_ssem, x_rsem, y_ssem, y_rsem, f_ssem, f_rsem, out_sem):
+                 w_sem, k_sem, v_sem, xin_sem, a_sem, kv_sem, c_ssem, c_rsem, x_ssem, x_rsem, y_ssem, y_rsem, f_ssem, f_rsem, out_sem):
     tp_id = lax.axis_index("tp")
     cp_id = lax.axis_index("cp")
     chip_x = cp_id // 2
@@ -230,7 +186,12 @@
     w_copies = [pltpu.make_async_copy(wu_hbm, wu, w_sem.at[1]), pltpu.make_async_copy(wd_hbm, wd, w_sem.at[2])]
     for head in range(HEADS):
         w_copies.append(pltpu.make_async_copy(wo_hbm.at[pl.ds(head * HEAD_DIM, HEAD_DIM)], wo.at[pl.ds((head % 2) * QUAD + (head // 2) * HEAD_DIM, HEAD_DIM)], w_sem.at[3 + head]))
-    side_copies = (pltpu.make_async_copy(wkv, wkv_hbm, side_sem.at[0]), pltpu.make_async_copy(trig, trig_hbm, side_sem.at[1]))
+
+    def a_back(g):
+        return [pltpu.make_async_copy(a_hbm.at[row_of(g, slot)], x_buf.at[g % 2, slot], xin_sem.at[g % 2, slot]) for slot in range(GROUP)]
+
+    def kv_put(g):
+        return [pltpu.make_async_copy(x_buf.at[g % 2, slot], kv_hbm.at[row_of(g, slot)], kv_sem.at[g % 2, slot]) for slot in range(GROUP)]
 
     def c_copies(g):
         return (remote(o_buf.at[g, pl.ds(4, 4)], c_recv.at[g], c_ssem.at[g, 0], c_rsem.at[g, 0], to_core), remote(stat.at[g, 0], c_stat.at[g], c_ssem.at[g, 1], c_rsem.at[g, 1], to_core))
@@ -318,6 +279,11 @@
             both = jnp.dot(vbuf[(g * GROUP + j) % V_BUFS, pair * PAIR:(pair + 1) * PAIR, :], p_buf[:, sub * PAIR:(sub + 1) * PAIR], preferred_element_type=F32)
             o_buf[g, slot, pair * HEAD_DIM:(pair + 1) * HEAD_DIM, :] = jnp.where(low_half, both[:HEAD_DIM], both[HEAD_DIM:])
 
+    def when_group(g, work):
+        @pl.when(jnp.logical_and(g >= 0, g < GROUPS))
+        def _():
+            work(g)
+
     def attend_group(g):
         first = g * GROUP
 
@@ -358,6 +324,7 @@
             def _():
                 for copy in c_copies(g):
                     copy.start()
+                when_group(g - FORWARD_LAG, forward_stage)
 
             return carry
 
@@ -420,6 +387,25 @@
         mlp_acc[...] = jnp.dot(hidden, wd[...], preferred_element_type=F32)
         y_keep[g % 3] = x_both[:CHUNK] + bo_ref[...].astype(F32).reshape(1, D_MODEL) + bd_ref[...].astype(F32).reshape(1, D_MODEL)
 
+    def keys_values(g):
+        b = g % 2
+        for copy in a_back(g):
+            copy.wait()
+        for half in range(2):
+            first = half * HALF
+            a = x_buf[b, first:first + HALF].reshape(HALF * CHUNK, D_MODEL)
+            kv = (jnp.dot(a, wkv[...], preferred_element_type=F32) + bias_kv[...]).astype(BF16)
+            for pair in range(HEADS // 2):
+                cols = slice(pair * PAIR, (pair + 1) * PAIR)
+                turned = jnp.dot(kv[:, cols], rot_ref[...], preferred_element_type=F32)
+                for k in range(HALF):
+                    tokens = slice(k * CHUNK, (k + 1) * CHUNK)
+                    x_buf[b, first + k, :, cols] = rotate(kv[tokens, cols], turned[tokens], row_tables(trig, row_of(g, first + k)), 1.0)
+            for k in range(HALF):
+                x_buf[b, first + k, :, WIDTH:] = kv[k * CHUNK:(k + 1) * CHUNK, WIDTH:]
+        for copy in kv_put(g):
+            copy.start()
+
     def x_stage(g):
         for copy in x_copies(g):
             copy.wait_recv()
@@ -490,11 +476,6 @@
             stage[g % 2, slot] = fin[g, slot].astype(BF16)
             out_copy(g, slot).start()
 
-    def when_group(g, work):
-        @pl.when(jnp.logical_and(g >= 0, g < GROUPS))
-        def _():
-            work(g)
-
     wqkv_copy.start()
     for copy in x_in(0):
         copy.start()
@@ -541,8 +522,6 @@
     lax.fori_loop(0, D_MODEL // PAIR, arrange, 0)
     for copy in w_copies:
         copy.start()
-    for copy in side_copies:
-        copy.start()
     pl.semaphore_wait(barrier, 3)
 
     def iteration(i, carry):
@@ -551,7 +530,24 @@
             for copy in x_in(i + 1):
                 copy.start()
 
+        @pl.when(i == GROUPS)
+        def _():
+            for half in range(2):
+                for copy in a_copies(GROUPS - 1, half):
+                    copy.wait()
+
+        @pl.when(jnp.logical_and(i > GROUPS, i < 2 * GROUPS))
+        def _():
+            for copy in kv_put(i - 1 - GROUPS):
+                copy.wait()
+
+        @pl.when(jnp.logical_and(i + 1 >= GROUPS, i + 1 < 2 * GROUPS))
+        def _():
+            for copy in a_back(i + 1 - GROUPS):
+                copy.start()
+
         when_group(i - DIAGONAL_LAG, diagonal_stage)
+        when_group(i - GROUPS, keys_values)
 
         @pl.when(i < GROUPS)
         def _():
@@ -562,10 +558,12 @@
             attend_group(i)
             core_stage(i)
 
+        @pl.when(i >= GROUPS)
+        def _():
+            when_group(i - FORWARD_LAG, forward_stage)
+
+        when_group(i - OUT_LAG, out_stage)
         when_group(i - 1, x_stage)
-        when_group(i - FORWARD_LAG, forward_stage)
-        when_group(i - DIAGONAL_LAG, out_stage)
-        when_group(i - 2, y_stage)
 
         @pl.when(i == 0)
         def _():
@@ -573,14 +571,12 @@
                 copy.wait()
 
         when_group(i, prepare)
+        when_group(i - 2, y_stage)
         return carry
 
-    lax.fori_loop(0, GROUPS + DIAGONAL_LAG, iteration, 0)
-    for copy in side_copies:
+    lax.fori_loop(0, GROUPS + OUT_LAG, iteration, 0)
+    for copy in kv_put(GROUPS - 1):
         copy.wait()
-    for half in range(2):
-        for copy in a_copies(GROUPS - 1, half):
-            copy.wait()
     for g in (GROUPS - 2, GROUPS - 1):
         for slot in range(GROUP):
             out_copy(g, slot).wait()
@@ -601,12 +597,11 @@
     return pl.pallas_call(
         layer_kernel,
         in_specs=[pl.BlockSpec(memory_space=pltpu.SMEM), ANY, ANY, ANY, vmem, vmem, vmem, vmem, ANY, vmem, vmem, ANY, ANY, vmem, ANY, vmem, vmem],
-        out_specs=[ANY, ANY, ANY, ANY],
+        out_specs=[ANY, ANY, ANY],
         out_shape=[
             jax.ShapeDtypeStruct((ROWS, CHUNK, D_MODEL), BF16),
             jax.ShapeDtypeStruct((ROWS, CHUNK, D_MODEL), BF16),
-            jax.ShapeDtypeStruct((D_MODEL, 2 * WIDTH), BF16),
-            jax.ShapeDtypeStruct((4, CHUNK, PAIR), F32),
+            jax.ShapeDtypeStruct((ROWS, CHUNK, D_MODEL), BF16),
         ],
         scratch_shapes=[
             pltpu.VMEM((WIDTH, D_MODEL), BF16),
@@ -643,7 +638,7 @@
             pltpu.VMEM((GROUPS, CHUNK, D_MODEL), F32),
             pltpu.VMEM((GROUPS, GROUP, CHUNK, D_MODEL), F32),
             pltpu.VMEM((2, GROUP, CHUNK, D_MODEL), BF16),
-            dma((3 + HEADS,)), dma((K_BUFS,)), dma((V_BUFS,)), dma((2, GROUP)), dma((2, HALF)), dma((2,)),
+            dma((3 + HEADS,)), dma((K_BUFS,)), dma((V_BUFS,)), dma((2, GROUP)), dma((2, HALF)), dma((2, GROUP)),
             dma((GROUPS, 2)), dma((GROUPS, 2)), dma((GROUPS, 2)), dma((GROUPS, 2)),
             dma((GROUPS,)), dma((GROUPS,)), dma((GROUPS, 7)), dma((GROUPS, GROUP)), dma((2, GROUP)),
         ],
@@ -660,9 +655,7 @@
     def local_layer(hidden_in, lengths, k_block, v_block, ln1_gain, ln1_bias, ln2_gain, ln2_bias, w_qkv, b_qkv, w_out, b_out, w_up, b_up, w_down, b_down):
         slot_minor = lambda cache: jnp.swapaxes(cache, 2, 3).reshape(ROWS, WIDTH, SLOTS)
         rot = jnp.asarray(rotate_matrix(), BF16)
-        through, normed, w_kv, trig = layer_call(lengths, slot_minor(k_block), slot_minor(v_block), hidden_in, ln1_gain, ln1_bias, ln2_gain, ln2_bias, w_qkv, b_qkv, rot, w_out, w_up, b_up, w_down, b_out, b_down)
-        flat = lambda values: values.reshape(ROWS * CHUNK, D_MODEL)
-        out, k_new, v_new = tail_call(flat(normed), w_kv, b_qkv, trig, rot, flat(through))
-        return out.reshape(ROWS, CHUNK, D_MODEL), k_new, v_new
+        through, _, kv = layer_call(lengths, slot_minor(k_block), slot_minor(v_block), hidden_in, ln1_gain, ln1_bias, ln2_gain, ln2_bias, w_qkv, b_qkv, rot, w_out, w_up, b_up, w_down, b_out, b_down)
+        return tail_call(kv, through)
 
     return jax.shard_map(local_layer, mesh=mesh, in_specs=in_specs, out_specs=out_specs, check_vma=False)

time: 175 us -> 168 us (0.960)
  Pallas kernels: 173 us -> 165 us
    pallas_call x1, Pallas kernels: 22.5 us -> 14.5 us  [tail_call(): pl.pallas_call(tail_kernel, in_specs=[ANY, ANY], out_specs=[ANY, ANY, ANY...]
where the time goes in v4:
time: 168 us; the launch traced here: 166 us
  Pallas kernels  165 us (98%)
    pallas_call x1, Pallas kernels, layer_call(): pl.pallas_call(layer_kernel, in_specs=[pl.BlockSpec(memory_space=pltpu.SM...  150 us
    pallas_call x1, Pallas kernels, tail_call(): pl.pallas_call(tail_kernel, in_specs=[ANY, ANY], out_specs=[ANY, ANY, ANY...  14.5 us

profile of v4, /device:TPU:1, one launch (start us, length us, event | category | flops | bytes accessed | tf_op | source)
XLA Modules:
  0.0 165.6 jit_solution(16477531924214537667)
XLA Ops:
  0.6 150.5 %layer.1 = (bf16[64,64,1024]{2,1,0:T(8,128)(2,1)}, bf16[64,64,1024]{2,1,0:T(8,128)(2,1)}, bf16[64,64,1024]{2,1,0:T(8,128)(2,1)}) custom-call(s32[64]{0:T(128)} %len_ref.1, bf16[64,512,512]{2,1,0:T(8,128)(2,1)} %bitcast.6, bf16[64,512,512]{2,1,0:T(8,128)(2,1)} %bitcast.7, bf16[64,64,1024]{2,1,0:T(8,128)(2,1)} %x_hbm.1, f32[1024]{0:T(1024)} %gain1_ref.1, ...), custom_call_target="tpu_custom_call" | custom-call | flops 30000001024 | bytes 104857600 | tf_op jit(solution)/shard_map/layer/pallas_call | solution.py:597
  151.1 14.5 %tail.1 = (bf16[64,64,1024]{2,1,0:T(8,128)(2,1)}, bf16[64,8,64,64]{3,2,1,0:T(8,128)(2,1)}, bf16[64,8,64,64]{3,2,1,0:T(8,128)(2,1)}) custom-call(bf16[64,64,1024]{2,1,0:T(8,128)(2,1)} %get-tuple-element.5.kv_hbm, bf16[64,64,1024]{2,1,0:T(8,128)(2,1)} %get-tuple-element.6.through_hbm), custom_call_target="tpu_custom_call" | custom-call | flops 1048576 | bytes 44040192 | tf_op jit(solution)/shard_map/tail/pallas_call | solution.py:128

commit v5 on v4

--- a/solution.py
+++ b/solution.py
@@ -28,11 +28,13 @@
 AHEAD = 2
 STRIP = 64
 FORWARD_LAG = 5
-DIAGONAL_LAG = 8
+DIAGONAL_LAG = 9
 OUT_LAG = 9
 QUAD = 4 * HEAD_DIM
 HALF = GROUP // 2
 TAIL_ROWS = 4
+STATS = 4 * HEAD_DIM
+SLAB = STATS + 8
 TAIL_SLOTS = 4
 F32 = jnp.float32
 BF16 = jnp.bfloat16
@@ -150,8 +152,8 @@
 def layer_kernel(len_ref, kc_hbm, vc_hbm, x_hbm, gain1_ref, bias1_ref, gain2_ref, bias2_ref, wqkv_hbm, bq_ref, rot_ref, wo_hbm, wu_hbm, bu_ref, wd_hbm, bo_ref, bd_ref,
                  out_hbm, a_hbm, kv_hbm,
                  wo, wu, wd, wq, wkv, bias_q, bias_kv, trig, kbuf, vbuf, s0, s1, p0, p1, x_buf, a_buf, q_buf, kv_self, own_o, own_stat, mlp_acc,
-                 o_buf, stat, c_recv, c_stat, cx_stat, x_recv, x_stat, ctx, y_send, y_keep, y_recv, fin, stage,
-                 w_sem, k_sem, v_sem, xin_sem, a_sem, kv_sem, c_ssem, c_rsem, x_ssem, x_rsem, y_ssem, y_rsem, f_ssem, f_rsem, out_sem):
+                 o_buf, c_recv, x_recv, ctx, y_send, y_keep, y_recv, fin, stage,
+                 w_sem, k_sem, v_sem, xin_sem, a_sem, kv_sem, send_sem, c_rsem, x_rsem, y_rsem, f_rsem, out_sem):
     tp_id = lax.axis_index("tp")
     cp_id = lax.axis_index("cp")
     chip_x = cp_id // 2
@@ -176,37 +178,52 @@
         return (pltpu.make_async_copy(kc_hbm.at[row], kbuf.at[kb], k_sem.at[kb]), pltpu.make_async_copy(vc_hbm.at[row], vbuf.at[vb], v_sem.at[vb]))
 
     def x_in(g):
-        return [pltpu.make_async_copy(x_hbm.at[row_of(g, slot)], x_buf.at[g % 2, slot], xin_sem.at[g % 2, slot]) for slot in range(GROUP)]
+        return [pltpu.make_async_copy(x_hbm.at[row_of(g, slot)], x_buf.at[g % 2, slot], xin_sem.at[g % 2]) for slot in range(GROUP)]
 
     def a_copies(g, half):
         first = 4 - 4 * half
-        return [pltpu.make_async_copy(a_buf.at[half, pl.ds(k * CHUNK, CHUNK)], a_hbm.at[row_of(g, first + k)], a_sem.at[half, k]) for k in range(HALF)]
+        return [pltpu.make_async_copy(a_buf.at[half, k], a_hbm.at[row_of(g, first + k)], a_sem.at[half]) for k in range(HALF)]
 
     wqkv_copy = pltpu.make_async_copy(wqkv_hbm, wu.at[:, pl.ds(0, 3 * WIDTH)], w_sem.at[0])
     w_copies = [pltpu.make_async_copy(wu_hbm, wu, w_sem.at[1]), pltpu.make_async_copy(wd_hbm, wd, w_sem.at[2])]
     for head in range(HEADS):
-        w_copies.append(pltpu.make_async_copy(wo_hbm.at[pl.ds(head * HEAD_DIM, HEAD_DIM)], wo.at[pl.ds((head % 2) * QUAD + (head // 2) * HEAD_DIM, HEAD_DIM)], w_sem.at[3 + head]))
+        w_copies.append(pltpu.make_async_copy(wo_hbm.at[pl.ds(head * HEAD_DIM, HEAD_DIM)], wo.at[pl.ds((head % 2) * QUAD + (head // 2) * HEAD_DIM, HEAD_DIM)], w_sem.at[3]))
 
     def a_back(g):
-        return [pltpu.make_async_copy(a_hbm.at[row_of(g, slot)], x_buf.at[g % 2, slot], xin_sem.at[g % 2, slot]) for slot in range(GROUP)]
+        return [pltpu.make_async_copy(a_hbm.at[row_of(g, slot)], x_buf.at[g % 2, slot], xin_sem.at[g % 2]) for slot in range(GROUP)]
+
+    def x_arrived(g):
+        pltpu.make_async_copy(x_hbm.at[pl.ds(0, GROUP)], x_buf.at[g % 2], xin_sem.at[g % 2]).wait()
+
+    def a_written(half):
+        pltpu.make_async_copy(a_buf.at[half], a_hbm.at[pl.ds(0, HALF)], a_sem.at[half]).wait()
+
+    def kv_written(g):
+        pltpu.make_async_copy(x_buf.at[g % 2], kv_hbm.at[pl.ds(0, GROUP)], kv_sem.at[g % 2]).wait()
+
+    def out_written():
+        pltpu.make_async_copy(stage, out_hbm.at[pl.ds(0, GROUP)], out_sem.at[0]).wait()
 
     def kv_put(g):
-        return [pltpu.make_async_copy(x_buf.at[g % 2, slot], kv_hbm.at[row_of(g, slot)], kv_sem.at[g % 2, slot]) for slot in range(GROUP)]
+        return [pltpu.make_async_copy(x_buf.at[g % 2, slot], kv_hbm.at[row_of(g, slot)], kv_sem.at[g % 2]) for slot in range(GROUP)]
 
     def c_copies(g):
-        return (remote(o_buf.at[g, pl.ds(4, 4)], c_recv.at[g], c_ssem.at[g, 0], c_rsem.at[g, 0], to_core), remote(stat.at[g, 0], c_stat.at[g], c_ssem.at[g, 1], c_rsem.at[g, 1], to_core))
+        return (remote(o_buf.at[g, pl.ds(4, 4)], c_recv.at[g], send_sem.at[0], c_rsem.at[g], to_core),)
 
     def x_copies(g):
-        return (remote(o_buf.at[g, pl.ds(2, 2)], x_recv.at[g], x_ssem.at[g, 0], x_rsem.at[g, 0], to_x), remote(cx_stat.at[g, pl.ds(2, 2)], x_stat.at[g], x_ssem.at[g, 1], x_rsem.at[g, 1], to_x))
+        return (remote(o_buf.at[g, pl.ds(2, 2)], x_recv.at[g], send_sem.at[1], x_rsem.at[g], to_x),)
 
     def y_copy(g):
-        return remote(y_send.at[g], y_recv.at[g], y_ssem.at[g], y_rsem.at[g], to_y)
-
-    def f_copy(g, src, dst, k, device):
-        return remote(fin.at[g, src], fin.at[g, dst], f_ssem.at[g, k], f_rsem.at[g, dst], device)
+        return remote(y_send.at[g], y_recv.at[g], send_sem.at[2], y_rsem.at[g], to_y)
+
+    def f_copy(g, src, dst, device):
+        return remote(fin.at[g, src], fin.at[g, dst], send_sem.at[3], f_rsem.at[g, min(dst, 4)], device)
+
+    def from_core(g):
+        return remote(fin.at[g, pl.ds(0, 4)], fin.at[g, pl.ds(4, 4)], send_sem.at[3], f_rsem.at[g, 4], to_core)
 
     def out_copy(g, slot):
-        return pltpu.make_async_copy(stage.at[g % 2, slot], out_hbm.at[row_of(g, slot)], out_sem.at[g % 2, slot])
+        return pltpu.make_async_copy(stage.at[slot], out_hbm.at[row_of(g, slot)], out_sem.at[0])
 
     lane = lax.broadcasted_iota(jnp.int32, (CHUNK, PAIR), 1)
     low_half = lane < HEAD_DIM
@@ -225,12 +242,11 @@
 
         @pl.when(g >= 1)
         def _():
-            for copy in a_copies(g - 1, half):
-                copy.wait()
+            a_written(half)
 
         x = x_buf[g % 2, first:first + HALF].reshape(HALF * CHUNK, D_MODEL).astype(F32)
         normed = normalize(x, gain1_ref[...].reshape(1, D_MODEL), bias1_ref[...].reshape(1, D_MODEL))
-        a_buf[half] = normed
+        a_buf[half] = normed.reshape(HALF, CHUNK, D_MODEL)
         for copy in a_copies(g, half):
             copy.start()
         q_all = (jnp.dot(normed, wq[...], preferred_element_type=F32) + bias_q[...]).astype(BF16)
@@ -269,8 +285,8 @@
         for sub in range(2):
             pair = 2 * quad + sub
             cols = slice(sub * PAIR, (sub + 1) * PAIR)
-            stat[g, j // HALF, j % HALF, pair:pair + 1, :] = top[:, cols]
-            stat[g, j // HALF, j % HALF, 4 + pair:5 + pair, :] = total[:, cols]
+            o_buf[g, slot_at(j), STATS + pair:STATS + pair + 1, :] = top[:, cols]
+            o_buf[g, slot_at(j), STATS + 4 + pair:STATS + 5 + pair, :] = total[:, cols]
 
     def value_unit(g, j, quad, p_buf):
         slot = slot_at(j)
@@ -337,13 +353,13 @@
         for copy in c_copies(g):
             copy.wait_recv()
         for slot in (2, 3, 0, 1):
-            mine = stat[g, 1, slot]
-            theirs = c_stat[g, slot]
+            mine = o_buf[g, slot, STATS:, :]
+            theirs = c_recv[g, slot, STATS:, :]
             top = jnp.maximum(mine, theirs)
             w_mine = jnp.exp(mine - top)
             w_theirs = jnp.exp(theirs - top)
             total = mine * pltpu.roll(w_mine, 4, 0) + theirs * pltpu.roll(w_theirs, 4, 0)
-            cx_stat[g, slot] = jnp.where(is_max, top, total)
+            o_buf[g, slot, STATS:, :] = jnp.where(is_max, top, total)
             for pair in range(HEADS // 2):
                 dims = slice(pair * HEAD_DIM, (pair + 1) * HEAD_DIM)
                 o_buf[g, slot, dims, :] = o_buf[g, slot, dims, :] * w_mine[pair:pair + 1] + c_recv[g, slot, dims, :] * w_theirs[pair:pair + 1]
@@ -352,7 +368,7 @@
                     copy.start()
 
     def prepare(g):
-        kv = (jnp.dot(a_buf[1, :2 * CHUNK], wkv[...], preferred_element_type=F32) + bias_kv[...]).astype(BF16)
+        kv = (jnp.dot(a_buf[1, :2].reshape(2 * CHUNK, D_MODEL), wkv[...], preferred_element_type=F32) + bias_kv[...]).astype(BF16)
         tables = [row_tables(trig, row_of(g, slot)) for slot in range(2)]
         for pair in range(HEADS // 2):
             cols = slice(pair * PAIR, (pair + 1) * PAIR)
@@ -389,8 +405,7 @@
 
     def keys_values(g):
         b = g % 2
-        for copy in a_back(g):
-            copy.wait()
+        x_arrived(g)
         for half in range(2):
             first = half * HALF
             a = x_buf[b, first:first + HALF].reshape(HALF * CHUNK, D_MODEL)
@@ -410,8 +425,8 @@
         for copy in x_copies(g):
             copy.wait_recv()
         for slot in range(2):
-            mine = cx_stat[g, slot]
-            theirs = x_stat[g, slot]
+            mine = o_buf[g, slot, STATS:, :]
+            theirs = x_recv[g, slot, STATS:, :]
             own = own_stat[slot]
             top = jnp.maximum(jnp.maximum(mine, theirs), own)
             w_mine = jnp.exp(mine - top)
@@ -438,50 +453,43 @@
     def y_stage(g):
         y_copy(g).wait_recv()
         fin[g, 0] = y_keep[g % 3] + y_recv[g]
-        f_copy(g, 0, 2, 0, to_x).start()
-        f_copy(g, 0, 1, 1, to_y).start()
-        f_copy(g, 0, 4, 2, to_core).start()
+        f_copy(g, 0, 2, to_x).start()
+        f_copy(g, 0, 1, to_y).start()
+        f_copy(g, 0, 4, to_core).start()
 
     def forward_stage(g):
-        f_copy(g, 0, 1, 1, to_y).wait_recv()
-        f_copy(g, 0, 2, 0, to_x).wait_recv()
+        f_copy(g, 0, 1, to_y).wait_recv()
+        f_copy(g, 0, 2, to_x).wait_recv()
 
         @pl.when(g % 2 == 0)
         def _():
-            f_copy(g, 1, 3, 3, to_x).start()
+            f_copy(g, 1, 3, to_x).start()
 
         @pl.when(g % 2 == 1)
         def _():
-            f_copy(g, 2, 3, 3, to_y).start()
-
-        f_copy(g, 1, 5, 4, to_core).start()
-        f_copy(g, 2, 6, 5, to_core).start()
+            f_copy(g, 2, 3, to_y).start()
+
+        f_copy(g, 1, 5, to_core).start()
+        f_copy(g, 2, 6, to_core).start()
 
     def diagonal_stage(g):
-        f_copy(g, 1, 3, 3, to_x).wait_recv()
-        f_copy(g, 3, 7, 6, to_core).start()
+        f_copy(g, 1, 3, to_x).wait_recv()
+        f_copy(g, 3, 7, to_core).start()
 
     def out_stage(g):
-        f_copy(g, 0, 4, 2, to_core).wait_recv()
-        f_copy(g, 1, 5, 4, to_core).wait_recv()
-        f_copy(g, 2, 6, 5, to_core).wait_recv()
-        f_copy(g, 3, 7, 6, to_core).wait_recv()
-
-        @pl.when(g >= 2)
-        def _():
-            for slot in range(GROUP):
-                out_copy(g - 2, slot).wait()
+        from_core(g).wait_recv()
+
+        @pl.when(g >= 1)
+        def _():
+            out_written()
 
         for slot in range(GROUP):
-            stage[g % 2, slot] = fin[g, slot].astype(BF16)
+            stage[slot] = fin[g, slot].astype(BF16)
             out_copy(g, slot).start()
 
     wqkv_copy.start()
     for copy in x_in(0):
         copy.start()
-    for n in range(AHEAD):
-        for copy in kv_copies(n):
-            copy.start()
     barrier = pltpu.get_barrier_semaphore()
     for device in (to_core, to_x, to_y):
         pl.semaphore_signal(barrier, inc=1, device_id=device, device_id_type=pl.DeviceIdType.MESH)
@@ -508,6 +516,9 @@
     bias_kv[:, :WIDTH] = k_bias
     bias_kv[:, WIDTH:] = v_bias
     wqkv_copy.wait()
+    for n in range(AHEAD):
+        for copy in kv_copies(n):
+            copy.start()
 
     def arrange(r, carry):
         rows = pl.ds(pl.multiple_of(r * PAIR, PAIR), PAIR)
@@ -533,13 +544,11 @@
         @pl.when(i == GROUPS)
         def _():
             for half in range(2):
-                for copy in a_copies(GROUPS - 1, half):
-                    copy.wait()
+                a_written(half)
 
         @pl.when(jnp.logical_and(i > GROUPS, i < 2 * GROUPS))
         def _():
-            for copy in kv_put(i - 1 - GROUPS):
-                copy.wait()
+            kv_written(i - 1 - GROUPS)
 
         @pl.when(jnp.logical_and(i + 1 >= GROUPS, i + 1 < 2 * GROUPS))
         def _():
@@ -551,8 +560,7 @@
 
         @pl.when(i < GROUPS)
         def _():
-            for copy in x_in(i):
-                copy.wait()
+            x_arrived(i)
             project(i, 0)
             project(i, 1)
             attend_group(i)
@@ -567,28 +575,22 @@
 
         @pl.when(i == 0)
         def _():
-            for copy in w_copies:
+            for copy in w_copies[:2]:
                 copy.wait()
+            pltpu.make_async_copy(wo_hbm, wo, w_sem.at[3]).wait()
 
         when_group(i, prepare)
         when_group(i - 2, y_stage)
         return carry
 
     lax.fori_loop(0, GROUPS + OUT_LAG, iteration, 0)
-    for copy in kv_put(GROUPS - 1):
-        copy.wait()
-    for g in (GROUPS - 2, GROUPS - 1):
-        for slot in range(GROUP):
-            out_copy(g, slot).wait()
-
-    def finish(g, carry):
-        for copy in c_copies(g) + x_copies(g) + (y_copy(g),):
-            copy.wait_send()
-        for src, dst, k, device in ((0, 2, 0, to_x), (0, 1, 1, to_y), (0, 4, 2, to_core), (1, 3, 3, to_x), (1, 5, 4, to_core), (2, 6, 5, to_core), (3, 7, 6, to_core)):
-            f_copy(g, src, dst, k, device).wait_send()
-        return carry
-
-    lax.fori_loop(0, GROUPS, finish, 0)
+    kv_written(GROUPS - 1)
+    out_written()
+
+    remote(o_buf.at[pl.ds(0, GROUPS // 2)], o_buf.at[pl.ds(0, GROUPS // 2)], send_sem.at[0], c_rsem.at[0], to_core).wait_send()
+    remote(o_buf.at[pl.ds(0, GROUPS // 4)], o_buf.at[pl.ds(0, GROUPS // 4)], send_sem.at[1], x_rsem.at[0], to_x).wait_send()
+    remote(y_send, y_recv, send_sem.at[2], y_rsem.at[0], to_y).wait_send()
+    remote(fin.at[pl.ds(0, GROUPS - 1)], fin.at[pl.ds(0, GROUPS - 1)], send_sem.at[3], f_rsem.at[0, 0], to_x).wait_send()
 
 
 def layer_call(lengths, k_cache, v_cache, x, gain1, bias1, gain2, bias2, w_qkv, b_qkv, rot, w_out, w_up, b_up, w_down, b_out, b_down):
@@ -619,28 +621,23 @@
             pltpu.VMEM((SLOTS, QUAD), BF16),
             pltpu.VMEM((SLOTS, QUAD), BF16),
             pltpu.VMEM((2, GROUP, CHUNK, D_MODEL), BF16),
-            pltpu.VMEM((2, HALF * CHUNK, D_MODEL), BF16),
+            pltpu.VMEM((2, HALF, CHUNK, D_MODEL), BF16),
             pltpu.VMEM((GROUP, CHUNK, WIDTH), BF16),
             pltpu.VMEM((2, CHUNK, 2 * WIDTH), BF16),
             pltpu.VMEM((2, QUAD, PAIR), F32),
             pltpu.VMEM((2, 8, PAIR), F32),
             pltpu.VMEM((2 * CHUNK, D_MODEL), F32),
-            pltpu.VMEM((GROUPS, GROUP, QUAD, PAIR), F32),
-            pltpu.VMEM((GROUPS, 2, HALF, 8, PAIR), F32),
-            pltpu.VMEM((GROUPS, HALF, QUAD, PAIR), F32),
-            pltpu.VMEM((GROUPS, HALF, 8, PAIR), F32),
-            pltpu.VMEM((GROUPS, HALF, 8, PAIR), F32),
-            pltpu.VMEM((GROUPS, 2, QUAD, PAIR), F32),
-            pltpu.VMEM((GROUPS, 2, 8, PAIR), F32),
+            pltpu.VMEM((GROUPS, GROUP, SLAB, PAIR), F32),
+            pltpu.VMEM((GROUPS, HALF, SLAB, PAIR), F32),
+            pltpu.VMEM((GROUPS, 2, SLAB, PAIR), F32),
             pltpu.VMEM((2 * CHUNK, WIDTH), BF16),
             pltpu.VMEM((GROUPS, CHUNK, D_MODEL), F32),
             pltpu.VMEM((3, CHUNK, D_MODEL), F32),
             pltpu.VMEM((GROUPS, CHUNK, D_MODEL), F32),
             pltpu.VMEM((GROUPS, GROUP, CHUNK, D_MODEL), F32),
-            pltpu.VMEM((2, GROUP, CHUNK, D_MODEL), BF16),
-            dma((3 + HEADS,)), dma((K_BUFS,)), dma((V_BUFS,)), dma((2, GROUP)), dma((2, HALF)), dma((2, GROUP)),
-            dma((GROUPS, 2)), dma((GROUPS, 2)), dma((GROUPS, 2)), dma((GROUPS, 2)),
-            dma((GROUPS,)), dma((GROUPS,)), dma((GROUPS, 7)), dma((GROUPS, GROUP)), dma((2, GROUP)),
+            pltpu.VMEM((GROUP, CHUNK, D_MODEL), BF16),
+            dma((4,)), dma((K_BUFS,)), dma((V_BUFS,)), dma((2,)), dma((2,)), dma((2,)),
+            dma((4,)), dma((GROUPS,)), dma((GROUPS,)), dma((GROUPS,)), dma((GROUPS, 5)), dma((1,)),
         ],
         compiler_params=pltpu.CompilerParams(collective_id=0, has_side_effects=True, vmem_limit_bytes=67_000_000),
         cost_estimate=pl.CostEstimate(flops=30 * 10 ** 9, bytes_accessed=100 << 20, transcendentals=0),

time: 168 us -> 164 us (0.976)
  Pallas kernels: 165 us -> 162 us
    pallas_call x1, Pallas kernels: 150 us -> 148 us  [layer_call(): pl.pallas_call(layer_kernel, in_specs=[pl.BlockSpec(memory_space=pltpu.SM...]
where the time goes in v5:
time: 164 us; the launch traced here: 163 us
  Pallas kernels  162 us (99%)
    pallas_call x1, Pallas kernels, layer_call(): pl.pallas_call(layer_kernel, in_specs=[pl.BlockSpec(memory_space=pltpu.SM...  148 us
    pallas_call x1, Pallas kernels, tail_call(): pl.pallas_call(tail_kernel, in_specs=[ANY, ANY], out_specs=[ANY, ANY, ANY...  14.5 us

profile of v5, /device:TPU:1, one launch (start us, length us, event | category | flops | bytes accessed | tf_op | source)
XLA Modules:
  0.0 163.0 jit_solution(8180890304472221869)
XLA Ops:
  0.6 147.9 %layer.1 = (bf16[64,64,1024]{2,1,0:T(8,128)(2,1)}, bf16[64,64,1024]{2,1,0:T(8,128)(2,1)}, bf16[64,64,1024]{2,1,0:T(8,128)(2,1)}) custom-call(s32[64]{0:T(128)} %len_ref.1, bf16[64,512,512]{2,1,0:T(8,128)(2,1)} %bitcast.6, bf16[64,512,512]{2,1,0:T(8,128)(2,1)} %bitcast.7, bf16[64,64,1024]{2,1,0:T(8,128)(2,1)} %x_hbm.1, f32[1024]{0:T(1024)} %gain1_ref.1, ...), custom_call_target="tpu_custom_call" | custom-call | flops 30000001024 | bytes 104857600 | tf_op jit(solution)/shard_map/layer/pallas_call | solution.py:599
  148.5 14.5 %tail.1 = (bf16[64,64,1024]{2,1,0:T(8,128)(2,1)}, bf16[64,8,64,64]{3,2,1,0:T(8,128)(2,1)}, bf16[64,8,64,64]{3,2,1,0:T(8,128)(2,1)}) custom-call(bf16[64,64,1024]{2,1,0:T(8,128)(2,1)} %get-tuple-element.5.kv_hbm, bf16[64,64,1024]{2,1,0:T(8,128)(2,1)} %get-tuple-element.6.through_hbm), custom_call_target="tpu_custom_call" | custom-call | flops 1048576 | bytes 44040192 | tf_op jit(solution)/shard_map/tail/pallas_call | solution.py:130

commit v6 on v5

--- a/solution.py
+++ b/solution.py
@@ -32,10 +32,10 @@
 OUT_LAG = 9
 QUAD = 4 * HEAD_DIM
 HALF = GROUP // 2
-TAIL_ROWS = 4
+TAIL_ROWS = 8
 STATS = 4 * HEAD_DIM
 SLAB = STATS + 8
-TAIL_SLOTS = 4
+TAIL_SLOTS = 2
 F32 = jnp.float32
 BF16 = jnp.bfloat16
 ANY = pl.BlockSpec(memory_space=pl.ANY)
@@ -88,8 +88,8 @@
         return pl.ds(i * TAIL_ROWS, TAIL_ROWS)
 
     kv_in = lambda i: pltpu.make_async_copy(kv_hbm.at[rows(i)], kv_all.at[i], kv_sem.at[i])
-    pass_in = lambda i: pltpu.make_async_copy(through_hbm.at[rows(i)], passing.at[i], in_sem.at[i])
-    pass_out = lambda i: pltpu.make_async_copy(passing.at[i], out_hbm.at[rows(i)], out_sem.at[i])
+    pass_in = lambda i: pltpu.make_async_copy(through_hbm.at[rows(i)], passing.at[rows(i)], in_sem.at[i])
+    pass_out = lambda i: pltpu.make_async_copy(passing.at[rows(i)], out_hbm.at[rows(i)], out_sem.at[0])
     k_put = lambda i: pltpu.make_async_copy(k_stage.at[i % TAIL_SLOTS], k_hbm.at[rows(i)], k_sem.at[i % TAIL_SLOTS])
     v_put = lambda i: pltpu.make_async_copy(v_stage.at[i % TAIL_SLOTS], v_hbm.at[rows(i)], v_sem.at[i % TAIL_SLOTS])
 
@@ -120,8 +120,7 @@
     for i in range(blocks - TAIL_SLOTS, blocks):
         k_put(i).wait()
         v_put(i).wait()
-    for i in range(blocks):
-        pass_out(i).wait()
+    pltpu.make_async_copy(passing, out_hbm, out_sem.at[0]).wait()
 
 
 def tail_call(kv, through):
@@ -138,10 +137,10 @@
         ],
         scratch_shapes=[
             pltpu.VMEM((blocks, TAIL_ROWS, CHUNK, D_MODEL), BF16),
-            pltpu.VMEM((blocks, TAIL_ROWS, CHUNK, D_MODEL), BF16),
+            pltpu.VMEM((ROWS, CHUNK, D_MODEL), BF16),
             pltpu.VMEM((TAIL_SLOTS, TAIL_ROWS, HEADS, CHUNK, HEAD_DIM), BF16),
             pltpu.VMEM((TAIL_SLOTS, TAIL_ROWS, HEADS, CHUNK, HEAD_DIM), BF16),
-            dma((blocks,)), dma((blocks,)), dma((blocks,)), dma((TAIL_SLOTS,)), dma((TAIL_SLOTS,)),
+            dma((blocks,)), dma((blocks,)), dma((1,)), dma((TAIL_SLOTS,)), dma((TAIL_SLOTS,)),
         ],
         cost_estimate=pl.CostEstimate(flops=1 << 20, bytes_accessed=42 << 20, transcendentals=0),
         compiler_params=pltpu.CompilerParams(vmem_limit_bytes=60_000_000),
@@ -477,13 +476,13 @@
         f_copy(g, 3, 7, to_core).start()
 
     def out_stage(g):
-        from_core(g).wait_recv()
-
         @pl.when(g >= 1)
         def _():
             out_written()
 
         for slot in range(GROUP):
+            if slot == 4:
+                from_core(g).wait_recv()
             stage[slot] = fin[g, slot].astype(BF16)
             out_copy(g, slot).start()
 

time: 164 us -> 164 us (level)
  no operation moved by 1% of the time
where the time goes in v6:
time: 164 us; the launch traced here: 163 us
  Pallas kernels  162 us (99%)
    pallas_call x1, Pallas kernels, layer_call(): pl.pallas_call(layer_kernel, in_specs=[pl.BlockSpec(memory_space=pltpu.SM...  148 us
    pallas_call x1, Pallas kernels, tail_call(): pl.pallas_call(tail_kernel, in_specs=[ANY, ANY], out_specs=[ANY, ANY, ANY...  14.3 us

profile of v6, /device:TPU:1, one launch (start us, length us, event | category | flops | bytes accessed | tf_op | source)
XLA Modules:
  0.0 162.6 jit_solution(3068506848261526309)
XLA Ops:
  0.6 147.7 %layer.1 = (bf16[64,64,1024]{2,1,0:T(8,128)(2,1)}, bf16[64,64,1024]{2,1,0:T(8,128)(2,1)}, bf16[64,64,1024]{2,1,0:T(8,128)(2,1)}) custom-call(s32[64]{0:T(128)} %len_ref.1, bf16[64,512,512]{2,1,0:T(8,128)(2,1)} %bitcast.6, bf16[64,512,512]{2,1,0:T(8,128)(2,1)} %bitcast.7, bf16[64,64,1024]{2,1,0:T(8,128)(2,1)} %x_hbm.1, f32[1024]{0:T(1024)} %gain1_ref.1, ...), custom_call_target="tpu_custom_call" | custom-call | flops 30000001024 | bytes 104857600 | tf_op jit(solution)/shard_map/layer/pallas_call | solution.py:598
  148.3 14.3 %tail.1 = (bf16[64,64,1024]{2,1,0:T(8,128)(2,1)}, bf16[64,8,64,64]{3,2,1,0:T(8,128)(2,1)}, bf16[64,8,64,64]{3,2,1,0:T(8,128)(2,1)}) custom-call(bf16[64,64,1024]{2,1,0:T(8,128)(2,1)} %get-tuple-element.5.kv_hbm, bf16[64,64,1024]{2,1,0:T(8,128)(2,1)} %get-tuple-element.6.through_hbm), custom_call_target="tpu_custom_call" | custom-call | flops 1048576 | bytes 44040192 | tf_op jit(solution)/shard_map/tail/pallas_call | solution.py:129
